TPU v7x, 256 devices: a whole 4x4x8 slice. The times are simulated.
256 devices in a mesh: row: 8 (over x, z_hi), col: 32 (over y, z_lo, core).
Axes of the slice: x: 4, y: 4, z: 8 (z_hi: 2, z_lo: 4; z = z_hi * 4 + z_lo), core: 2. Of those that a mesh axis runs over, the one named last changes fastest.
Arguments:
- symmetric: float32 [12288, 12288], P('row', 'col'), may hold values from -24 to 24, as said below
Outputs:
- reduced: float32 [12288, 12288], P('row', 'col')
Inputs may be any that keep to these rules, and one draw needn't show every extreme that they name: symmetric equals its transpose.
All inputs are finite; a program needn't handle non-finite values.
Results may differ from a plain program's by a relative error of at most 0.0001.
Values sent between devices are 32-bit elements; how exact they have to be, the bound alone decides.
No kernel may reach another device: no remote copies, remote signals or barrier semaphores. Data moves between devices by JAX's collectives and lax.ppermute only.
A program may use at most 64 MiB of HBM per device.

v0:
```python
import math

import jax
import jax.numpy as jnp
from jax import lax
from jax.experimental import pallas as pl
from jax.experimental.pallas import tpu as pltpu
from jax.sharding import Mesh
from jax.sharding import PartitionSpec as P


N = 12288
B = 256
ROW = ("x", "zh")
COL = ("y", "zl", "c")
ALL = ROW + COL
SIZES = {"x": 4, "zh": 2, "y": 4, "zl": 4, "c": 2}
HIGHEST = lax.Precision.HIGHEST
INTERPRET = False
STEP = 64


def contract(left_op, right_op, left_dim, right_dim, precision=HIGHEST):
    return lax.dot_general(
        left_op,
        right_op,
        (((left_dim,), (right_dim,)), ((), ())),
        precision=precision,
        preferred_element_type=jnp.float32,
    )


def shifted(value, axis, by):
    size = SIZES[axis]
    return lax.ppermute(value, axis, [(k, (k + by) % size) for k in range(size)])


def gather_over(value, axis, dim=0):
    size = SIZES[axis]
    me = lax.axis_index(axis)
    out = jnp.zeros(value.shape[:dim] + (size,) + value.shape[dim:], value.dtype)
    for by in range(size):
        part = value if by == 0 else shifted(value, axis, by)
        out = lax.dynamic_update_index_in_dim(out, part, (me - by) % size, dim)
    return out


def from_everyone(value, axis):
    size = lax.axis_size(axis)
    return lax.all_to_all(
        jnp.broadcast_to(value[None], (size, *value.shape)), axis, 0, 0, tiled=True
    )


def plane_gather(piece, tied=None):
    rows, width = piece.shape
    half = width // 2
    left = gather_over(piece[:, :half], "y")
    right = gather_over(piece[:, half:], "zl")
    if tied is not None:
        left, right, tied = lax.optimization_barrier((left, right, tied))
    left = gather_over(left, "zl", 1)
    right = gather_over(right, "y", 0)
    left = gather_over(left.reshape(16 * rows, half), "c")
    right = gather_over(right.reshape(16 * rows, half), "c")
    left, right = left.reshape(32 * rows, half), right.reshape(32 * rows, half)
    return (left, right) if tied is None else (left, right, tied)


def row_gather(value):
    return from_everyone(value, ROW).reshape(8 * value.shape[0], value.shape[1])


def plane_place(piece):
    core, rest = divmod(piece, 16)
    return (rest // 4) * 8 + (rest % 4) * 2 + core


TO_PLANE = [
    (r * 32 + j, (j // 4) * 32 + plane_place((j % 4) * 8 + r)) for r in range(8) for j in range(32)
]


def spread_strip(parts):
    total = None
    for r in range(8):
        moves = [(j, (j // 4) * 32 + plane_place((j % 4) * 8 + r)) for j in range(32)]
        got = lax.ppermute(parts[r], ALL, moves)
        total = got if total is None else total + got
    return total


def mxu(left, right, left_dim=1, right_dim=0):
    return contract(left, right, left_dim, right_dim)


PANEL = 8


def panel_columns(work, at):
    return [
        jnp.broadcast_to(work[:, at + k : at + k + 1], work.shape) for k in range(PANEL)
    ]


def small_chol_inverse(block):
    size = block.shape[0]
    work = jnp.concatenate([block, eye_of(size)], axis=1)
    rows = lax.broadcasted_iota(jnp.int32, (size, 2 * size), 0)
    for at in range(0, size, PANEL):
        columns = panel_columns(work, at)
        for a in range(PANEL):
            k = at + a
            root = lax.rsqrt(columns[a][k : k + 1, :])
            factor = columns[a] * root
            for b in range(a + 1, PANEL):
                columns[b] = columns[b] - factor * factor[at + b : at + b + 1, :]
            line = work[k : k + 1, :] * root
            updated = work - factor * line
            work = jnp.where(rows == k, line, jnp.where(rows > k, updated, work))
    return work[:, size:]


def small_inverse(block):
    size = block.shape[0]
    work = jnp.concatenate([block, eye_of(size)], axis=1)
    rows = lax.broadcasted_iota(jnp.int32, (size, 2 * size), 0)
    for at in range(0, size, PANEL):
        columns = panel_columns(work, at)
        for a in range(PANEL):
            k = at + a
            scale = 1.0 / columns[a][k : k + 1, :]
            factor = jnp.where(rows == k, 1.0, columns[a])
            keep = rows != k
            for b in range(a + 1, PANEL):
                top = columns[b][k : k + 1, :] * scale
                columns[b] = jnp.where(keep, columns[b], 0.0) - jnp.where(
                    keep, factor, -1.0
                ) * top
            line = work[k : k + 1, :] * scale
            work = jnp.where(keep, work - factor * line, line)
    return work[:, size:]


def eye_of(size):
    rows = lax.broadcasted_iota(jnp.int32, (size, size), 0)
    cols = lax.broadcasted_iota(jnp.int32, (size, size), 1)
    return jnp.where(rows == cols, 1.0, 0.0).astype(jnp.float32)


def turned_left(value, by):
    return pltpu.roll(value, (B - by) % B, 1)[:, :STEP]


def chol_kernel(gram_ref, upper_ref, inverse_ref, work):
    lanes = lax.broadcasted_iota(jnp.int32, (STEP, B), 1)
    work[:, :B] = gram_ref[...]
    work[:, B:] = eye_of(B)

    def step(block, carry):
        at = pl.multiple_of(block * STEP, STEP)
        own = work[pl.ds(at, STEP), :]
        inv = small_chol_inverse(turned_left(own[:, :B], at))
        lines = mxu(inv, own)
        work[pl.ds(at, STEP), :] = lines
        ahead = jnp.where(lanes >= at + STEP, lines[:, :B], 0.0)
        work[...] = work[...] - mxu(ahead, lines, 0, 0)
        return carry

    lax.fori_loop(0, B // STEP, step, 0)
    rows = lax.broadcasted_iota(jnp.int32, (B, B), 0)
    cols = lax.broadcasted_iota(jnp.int32, (B, B), 1)
    upper_ref[...] = jnp.where(cols >= rows, work[:, :B], 0.0)
    inverse_ref[...] = jnp.where(cols <= rows, work[:, B:], 0.0)


def t_kernel(lead_ref, inverse_ref, t_ref, work):
    tall = lax.broadcasted_iota(jnp.int32, (B, STEP), 0)
    work[:, :B] = eye_of(B) - mxu(lead_ref[...], inverse_ref[...], 1, 1)
    work[:, B:] = eye_of(B)

    def step(block, carry):
        at = pl.multiple_of(block * STEP, STEP)
        turned = turned_left(work[:, :B], at)
        own = work[pl.ds(at, STEP), :]
        inv = small_inverse(turned_left(own[:, :B], at))
        lines = mxu(inv, own)
        others = jnp.where((tall < at) | (tall >= at + STEP), turned, 0.0)
        work[...] = work[...] - mxu(others, lines)
        work[pl.ds(at, STEP), :] = lines
        return carry

    lax.fori_loop(0, B // STEP, step, 0)
    t_ref[...] = work[:, B:]


def on_squares(kernel, outputs, *operands):
    square = jax.ShapeDtypeStruct((B, B), jnp.float32)
    vmem = pl.BlockSpec(memory_space=pltpu.VMEM)
    return pl.pallas_call(
        kernel,
        out_shape=(square,) * outputs,
        in_specs=[vmem] * len(operands),
        out_specs=(vmem,) * outputs,
        scratch_shapes=[pltpu.VMEM((B, 2 * B), jnp.float32)],
        cost_estimate=pl.CostEstimate(
            flops=2_000_000_000, bytes_accessed=4 * B * B * 4, transcendentals=0
        ),
        interpret=INTERPRET,
    )(*operands)


def chol(gram):
    return on_squares(chol_kernel, 2, gram)


def t_inverse(lead, inverse):
    return on_squares(t_kernel, 1, lead, inverse)[0]


def dot(left, right, left_dim, right_dim):
    return lax.dot_general(
        left, right, (((left_dim,), (right_dim,)), ((), ())), preferred_element_type=jnp.float32
    )


def bf16_parts(value, count):
    parts = []
    for _ in range(count):
        part = value.astype(jnp.bfloat16)
        parts.append(part)
        value = value - part.astype(jnp.float32)
    return parts


PAIRS = {2: ((0, 0), (0, 1), (1, 0)), 3: ((0, 0), (0, 1), (1, 0), (1, 1), (0, 2), (2, 0))}


def lefts(value, count, dim):
    parts = bf16_parts(value, count)
    return jnp.concatenate([parts[a] for a, _ in PAIRS[count]], axis=dim)


def rights(value, count):
    parts = bf16_parts(value, count)
    return jnp.concatenate([parts[b] for _, b in PAIRS[count]], axis=0)


def products_kernel(tile_ref, left_ref, right_ref, gram_ref, out_ref):
    @pl.when(pl.program_id(0) == 0)
    def _():
        gram_ref[...] = jnp.zeros(gram_ref.shape, jnp.float32)
        out_ref[...] = jnp.zeros(out_ref.shape, jnp.float32)

    panel = jnp.concatenate([left_ref[...], right_ref[...]], axis=1)
    gram_ref[...] += dot(lefts(panel, 3, 0), rights(panel, 3), 0, 0)
    out_ref[...] += dot(lefts(tile_ref[...], 2, 0), rights(panel, 2), 0, 0)


def products(tile, left, right):
    rows_dev, cols_dev = tile.shape
    lines = 2 * B
    return pl.pallas_call(
        products_kernel,
        out_shape=(
            jax.ShapeDtypeStruct((B, B), jnp.float32),
            jax.ShapeDtypeStruct((cols_dev, B), jnp.float32),
        ),
        grid=(rows_dev // lines,),
        in_specs=[
            pl.BlockSpec((lines, cols_dev), lambda k: (k, 0)),
            pl.BlockSpec((lines, B // 2), lambda k: (k, 0)),
            pl.BlockSpec((lines, B // 2), lambda k: (k, 0)),
        ],
        out_specs=(
            pl.BlockSpec((B, B), lambda k: (0, 0)),
            pl.BlockSpec((cols_dev, B), lambda k: (0, 0)),
        ),
        cost_estimate=pl.CostEstimate(
            flops=6 * rows_dev * (cols_dev + 2 * B) * B,
            bytes_accessed=4 * rows_dev * (cols_dev + B),
            transcendentals=0,
        ),
        interpret=INTERPRET,
        name="products",
    )(tile, left, right)


def update_kernel(
    at_ref, tile_ref, pl_ref, pr_ref, ul_ref, ur_ref, f_ref, w_ref, tv_ref, r_ref, rt_ref, out_ref, factors
):
    row_at, col_at = at_ref[0], at_ref[1]
    step = pl.program_id(0)
    six = 6 * B

    @pl.when(step == 0)
    def _():
        factors[:six, :] = rights(f_ref[...], 3)
        factors[six:, :] = rights(tv_ref[...], 2)

    panel = jnp.concatenate([pl_ref[...], pr_ref[...]], axis=1)
    u_mat = jnp.concatenate([ul_ref[...], ur_ref[...]], axis=1)
    both = jnp.concatenate([lefts(panel, 3, 1), lefts(u_mat, 2, 1)], axis=1)
    out_ref[...] = tile_ref[...] - dot(both, factors[...], 1, 0)

    @pl.when((row_at == 0) & (step == 1))
    def _():
        out_ref[...] = out_ref[...] + w_ref[...]

    top = (row_at == 0) & (step == 0)

    @pl.when((col_at == 0) & jnp.logical_not(top))
    def _():
        out_ref[:, :B] = jnp.zeros((B, B), jnp.float32)

    @pl.when((col_at == 0) & (row_at == 0) & (step == 1))
    def _():
        out_ref[:, :B] = r_ref[...]

    @pl.when(top & (col_at == 0))
    def _():
        out_ref[:, B:] = rt_ref[:, : B // 2]

    @pl.when(top & (col_at == 1))
    def _():
        out_ref[:, : B // 2] = rt_ref[:, B // 2 :]
        out_ref[:, B // 2 :] = jnp.zeros((B, B), jnp.float32)

    @pl.when(top & (col_at >= 2))
    def _():
        out_ref[...] = jnp.zeros(out_ref.shape, jnp.float32)


def updated(at, tile, panel, u_mat, small, upper):
    rows_dev, cols_dev = tile.shape

    def whole(shape):
        return pl.BlockSpec(shape, lambda k, at: (0, 0))

    def lines(width):
        return pl.BlockSpec((B, width), lambda k, at: (k, 0))

    return pl.pallas_call(
        update_kernel,
        out_shape=jax.ShapeDtypeStruct(tile.shape, jnp.float32),
        grid_spec=pltpu.PrefetchScalarGridSpec(
            num_scalar_prefetch=1,
            grid=(rows_dev // B,),
            in_specs=[lines(cols_dev)]
            + [lines(B // 2)] * 4
            + [whole((B, cols_dev))] * 3
            + [whole((B, B))] * 2,
            out_specs=lines(cols_dev),
            scratch_shapes=[pltpu.VMEM((9 * B, cols_dev), jnp.bfloat16)],
        ),
        cost_estimate=pl.CostEstimate(
            flops=9 * 2 * rows_dev * cols_dev * B,
            bytes_accessed=4 * rows_dev * (2 * cols_dev + 2 * B),
            transcendentals=0,
        ),
        interpret=INTERPRET,
        name="update",
    )(at, tile, *panel, *u_mat, *small, upper, upper.T)


def per_device(tile):
    _, cols_dev = tile.shape
    row_at = lax.axis_index(ROW)
    col_at = lax.axis_index(COL)
    global_cols = col_at * cols_dev + jnp.arange(cols_dev, dtype=jnp.int32)
    band = jnp.arange(B, dtype=jnp.int32)
    zero = jnp.float32(0.0)

    place = (
        lax.axis_index("c") * 16 + lax.axis_index("y") * 4 + lax.axis_index("zl")
    )
    at = jnp.stack([row_at, col_at]).astype(jnp.int32)

    strip = jnp.where((global_cols >= B)[:, None], tile[:B, :].T, zero)
    panel_part = spread_strip(strip.reshape(8, -1, B))
    panel = plane_gather(panel_part)

    gram, product = products(tile, *panel)
    gram_slice = lax.dynamic_slice_in_dim(gram, place * 8, 8, 0)
    lead_slice = jnp.concatenate(
        [lax.dynamic_slice_in_dim(half, B + place * 8, 8, 0) for half in panel], axis=1
    )
    lead_slice = jnp.where(row_at == 0, lead_slice, zero)
    message = jnp.concatenate([gram_slice, lead_slice], axis=0)
    message = jnp.concatenate(
        [product.reshape(8, -1, B), jnp.broadcast_to(message[None], (8, 16, B))], axis=1
    )
    message = lax.all_to_all(message, ROW, 0, 0, tiled=True)
    message = message.sum(axis=0)
    product_part, message = message[:-16], message[-16:]
    message = from_everyone(from_everyone(message, ("y", "zl")), "c")
    message = message.reshape(32, 2, 8, B)
    gram = message[:, 0].reshape(B, B)
    lead = message[:, 1].reshape(B, B)

    both = jnp.concatenate([strip, tile[B : 2 * B, :].T], axis=1).reshape(8, -1, 2 * B)
    both, gram = lax.optimization_barrier((both, gram))
    both = lax.all_to_all(both, ROW, 0, 0, tiled=True)
    both = both.reshape(8, -1, 2 * B)[0]
    upper, inverse = chol(gram)

    u_part = contract(product_part, inverse, 1, 1) - both[:, B:]
    u_there = lax.ppermute(u_part, ALL, TO_PLANE)
    both_j = row_gather(jnp.concatenate([both[:, :B], u_part], axis=1))
    t_mat = t_inverse(lead, inverse)
    unit_j = (global_cols[:, None] - B == band[None, :]).astype(jnp.float32)
    reflector_j = contract(both_j[:, :B], inverse, 1, 1) - unit_j
    u_j = both_j[:, B:]

    core_part = contract(reflector_j, u_j, 0, 0).reshape(32, 8, B)
    u_there, core_part = lax.optimization_barrier((u_there, core_part))
    core_part = lax.all_to_all(core_part, COL, 0, 0, tiled=True)
    core_part = core_part.reshape(32, 8, B).sum(axis=0)
    u_left, u_right, core_part = plane_gather(u_there, core_part)
    core_sum = from_everyone(core_part, COL).reshape(B, B)
    middle = contract(contract(t_mat, core_sum, 1, 0), t_mat, 1, 1)

    t_reflector_trans = contract(t_mat, reflector_j, 0, 1)
    w_trans = contract(t_mat, u_j, 1, 1) - contract(middle, reflector_j, 1, 1)
    first_trans = contract(inverse, w_trans, 0, 0)
    return updated(
        at,
        tile,
        panel,
        (u_left, u_right),
        (first_trans, w_trans, t_reflector_trans),
        upper * jnp.float32(1.0 / math.sqrt(N)),
    )


def solution(mesh):
    split = Mesh(mesh.devices.reshape(4, 2, 4, 4, 2), ALL)
    return jax.shard_map(
        per_device,
        mesh=split,
        in_specs=(P(ROW, COL),),
        out_specs=P(ROW, COL),
        check_vma=False,
    )
```

profile of v0, /device:TPU:1, one launch (start us, length us, event | category | flops | bytes accessed | tf_op | source)
XLA Modules:
  0.0 255.3 jit_solution(16285831512628923400)
XLA Ops:
  1.5 7.6 %collective-permute-start.1 = (f32[48,256]{0,1:T(8,128)S(1)}, f32[48,256]{0,1:T(8,128)S(1)}, u32[]{:S(2)}, u32[]{:S(2)}) collective-permute-start(f32[48,256]{0,1:T(8,128)S(1)} %get-tuple-element.31), channel_id=1, source_target_pairs={{0,2},{1,18},{2,3},{3,19},{4,34},{5,50},{6,35},{7,51},{8,66},{9,82... | collective-permute-start | bytes 147464 | tf_op jit(solution)/shard_map/ppermute | solution.py:88
  9.0 9.3 %collective-permute-start.7 = (f32[48,256]{0,1:T(8,128)S(1)}, f32[48,256]{0,1:T(8,128)S(1)}, u32[]{:S(2)}, u32[]{:S(2)}) collective-permute-start(f32[48,256]{0,1:T(8,128)S(1)} %get-tuple-element.32), channel_id=1, source_target_pairs={{0,14},{1,30},{2,15},{3,31},{4,46},{5,62},{6,47},{7,63},{8,78},{9,... | collective-permute-start | bytes 147464 | tf_op jit(solution)/shard_map/ppermute | solution.py:88
  31.5 8.7 %collective-permute-done = f32[48,256]{0,1:T(8,128)S(1)} collective-permute-done((f32[48,256]{0,1:T(8,128)S(1)}, f32[48,256]{0,1:T(8,128)S(1)}, u32[]{:S(2)}, u32[]{:S(2)}) %collective-permute-start) | collective-permute-done | bytes 49184 | tf_op jit(solution)/shard_map/ppermute | solution.py:88
  42.4 4.7 %collective-permute-start.15 = (f32[48,128]{0,1:T(8,128)S(1)}, f32[48,128]{0,1:T(8,128)S(1)}, u32[]{:S(2)}, u32[]{:S(2)}) collective-permute-start(f32[48,128]{0,1:T(8,128)S(1)} %get-tuple-element.41), channel_id=1, source_target_pairs={{0,2},{2,4},{4,6},{6,0},{1,3},{3,5},{5,7},{7,1},{8,10},{10,12},{12... | collective-permute-start | bytes 73736 | tf_op jit(solution)/shard_map/ppermute | solution.py:35
  47.1 5.2 %collective-permute-start.9 = (f32[48,128]{0,1:T(8,128)S(1)}, f32[48,128]{0,1:T(8,128)S(1)}, u32[]{:S(2)}, u32[]{:S(2)}) collective-permute-start(f32[48,128]{0,1:T(8,128)S(1)} %get-tuple-element.44), channel_id=1, source_target_pairs={{0,16},{8,24},{16,0},{24,8},{1,17},{9,25},{17,1},{25,9},{2,18},{10... | collective-permute-start | bytes 73736 | tf_op jit(solution)/shard_map/ppermute | solution.py:35
  61.6 4.9 %collective-permute-done.18 = f32[4,48,128]{2,1,0:T(8,128)S(1)} collective-permute-done((f32[4,48,128]{2,1,0:T(8,128)S(1)}, f32[4,48,128]{2,1,0:T(8,128)S(1)}, u32[]{:S(2)}, u32[]{:S(2)}) %collective-permute-start.18) | collective-permute-done | bytes 98336 | tf_op jit(solution)/shard_map/ppermute | solution.py:35
  66.4 5.0 %collective-permute-done.19 = f32[4,48,128]{2,1,0:T(8,128)S(1)} collective-permute-done((f32[4,48,128]{2,1,0:T(8,128)S(1)}, f32[4,48,128]{2,1,0:T(8,128)S(1)}, u32[]{:S(2)}, u32[]{:S(2)}) %collective-permute-start.19) | collective-permute-done | bytes 98336 | tf_op jit(solution)/shard_map/ppermute | solution.py:35
  71.4 5.3 %collective-permute-start.21 = (f32[768,128]{1,0:T(8,128)S(1)}, f32[768,128]{1,0:T(8,128)S(1)}, u32[]{:S(2)}, u32[]{:S(2)}) collective-permute-start(f32[768,128]{1,0:T(8,128)S(1)} %bitcast.138), channel_id=1, source_target_pairs={{0,1},{1,0},{2,3},{3,2},{4,5},{5,4},{6,7},{7,6},{8,9},{9,8},{10,11... | collective-permute-start | bytes 1179656 | tf_op jit(solution)/shard_map/ppermute | solution.py:35
  79.8 5.2 %products.1 = (f32[256,256]{1,0:T(8,128)}, f32[384,256]{1,0:T(8,128)}) custom-call(f32[1536,384]{1,0:T(8,128)} %tile_ref.3, f32[1536,128]{1,0:T(8,128)} %bitcast.145, f32[1536,128]{1,0:T(8,128)} %bitcast.142), custom_call_target="tpu_custom_call" | custom-call | flops 2113929216 | bytes 3932160 | tf_op jit(solution)/shard_map/products/pallas_call | solution.py:263
  87.5 17.8 %all_to_all.36 = f32[8,64,256]{2,1,0:T(8,128)S(1)} all-to-all(f32[8,64,256]{2,1,0:T(8,128)S(1)} %pad_maximum_fusion.1), channel_id=1, replica_groups=mesh['x'=4,'zh'=2,'y'=4,'zl'=4,'c'=2] {'x','zh'}, dimensions={0} | all-to-all | bytes 1048576 | tf_op jit(solution)/shard_map/all_to_all | solution.py:393
  106.0 8.2 %all-to-all-start.1 = ((f32[16,16,256]{2,1,0:T(8,128)}), f32[16,16,256]{2,1,0:T(8,128)S(1)}, u32[]{:S(2)}, u32[]{:S(2)}) async-start(f32[16,16,256]{2,1,0:T(8,128)} %broadcast_in_dim.197), calls=%async_computation.1 | async-start | bytes 524288 | tf_op jit(solution)/shard_map/all_to_all | solution.py:50
  115.5 7.4 %all-to-all-done.1 = f32[16,16,256]{2,1,0:T(8,128)S(1)} async-done(((f32[16,16,256]{2,1,0:T(8,128)}), f32[16,16,256]{2,1,0:T(8,128)S(1)}, u32[]{:S(2)}, u32[]{:S(2)}) %all-to-all-start.1) | async-done | bytes 262176 | tf_op jit(solution)/shard_map/all_to_all | solution.py:50
  123.0 7.0 %all_to_all.35 = f32[2,16,16,256]{3,2,1,0:T(8,128)S(1)} all-to-all(f32[2,16,16,256]{3,2,1,0:T(8,128)S(1)} %broadcast_in_dim.198), channel_id=1, replica_groups=mesh['x'=4,'zh'=2,'y'=4,'zl'=4,'c'=2] {'c'}, dimensions={0} | all-to-all | bytes 1048576 | tf_op jit(solution)/shard_map/all_to_all | solution.py:50
  130.8 3.5 %all-to-all-start.3 = ((f32[8,48,512]{2,1,0:T(8,128)}), f32[8,48,512]{2,1,0:T(8,128)S(1)}, u32[]{:S(2)}, u32[]{:S(2)}) async-start(f32[8,48,512]{2,1,0:T(8,128)} %bitcast.33), calls=%async_computation.3 | async-start | bytes 1572864 | tf_op jit(solution)/shard_map/all_to_all | solution.py:403
  134.4 12.4 %shard_map.17 = (f32[256,256]{1,0:T(8,128)}, f32[256,256]{1,0:T(8,128)}) custom-call(f32[256,256]{1,0:T(8,128)} %get-tuple-element.18.gram_ref), custom_call_target="tpu_custom_call" | custom-call | flops 2000000000 | bytes 1048576 | tf_op jit(solution)/shard_map/pallas_call | solution.py:200
  146.8 8.4 %all-to-all-done.3 = f32[8,48,512]{2,1,0:T(8,128)S(1)} async-done(((f32[8,48,512]{2,1,0:T(8,128)}), f32[8,48,512]{2,1,0:T(8,128)S(1)}, u32[]{:S(2)}, u32[]{:S(2)}) %all-to-all-start.3) | async-done | bytes 786464 | tf_op jit(solution)/shard_map/all_to_all | solution.py:403
  157.5 3.5 %all-to-all-start.4 = ((f32[8,48,512]{2,1,0:T(8,128)}), f32[8,48,512]{2,1,0:T(8,128)S(1)}, u32[]{:S(2)}, u32[]{:S(2)}) async-start(f32[8,48,512]{2,1,0:T(8,128)} %broadcast_in_dim.199), calls=%async_computation.4 | async-start | bytes 1572864 | tf_op jit(solution)/shard_map/all_to_all | solution.py:50
  163.4 13.5 %shard_map.18 = f32[256,256]{1,0:T(8,128)} custom-call(f32[256,256]{1,0:T(8,128)} %get-tuple-element.29.lead_ref, f32[256,256]{1,0:T(8,128)} %get-tuple-element.19.inverse_ref), custom_call_target="tpu_custom_call" | custom-call | flops 2000000000 | bytes 1048576 | tf_op jit(solution)/shard_map/pallas_call | solution.py:200
  185.7 5.2 %collective-permute-start.27 = (f32[48,128]{1,0:T(8,128)S(1)}, f32[48,128]{1,0:T(8,128)S(1)}, u32[]{:S(2)}, u32[]{:S(2)}) collective-permute-start(f32[48,128]{1,0:T(8,128)S(1)} %get-tuple-element.45), channel_id=1, source_target_pairs={{0,4},{2,6},{4,0},{6,2},{1,5},{3,7},{5,1},{7,3},{8,12},{10,14},{12... | collective-permute-start | bytes 73736 | tf_op jit(solution)/shard_map/ppermute | solution.py:35
  200.4 8.2 %all-to-all-start.5 = ((f32[32,8,256]{2,1,0:T(8,128)}), f32[32,8,256]{2,1,0:T(8,128)S(1)}, u32[]{:S(2)}, u32[]{:S(2)}) async-start(f32[32,8,256]{2,1,0:T(8,128)} %convolution_bitcast_fusion), calls=%async_computation.5 | async-start | bytes 524288 | tf_op jit(solution)/shard_map/all_to_all | solution.py:417
  212.2 7.6 %all-to-all-done.5 = f32[32,8,256]{2,1,0:T(8,128)S(1)} async-done(((f32[32,8,256]{2,1,0:T(8,128)}), f32[32,8,256]{2,1,0:T(8,128)S(1)}, u32[]{:S(2)}, u32[]{:S(2)}) %all-to-all-start.5) | async-done | bytes 262176 | tf_op jit(solution)/shard_map/all_to_all | solution.py:417
  224.4 7.2 %all-to-all-start.6 = ((f32[32,8,256]{2,1,0:T(8,128)}), f32[32,8,256]{2,1,0:T(8,128)S(1)}, u32[]{:S(2)}, u32[]{:S(2)}) async-start(f32[32,8,256]{2,1,0:T(8,128)} %broadcast_in_dim.220), calls=%async_computation.6 | async-start | bytes 524288 | tf_op jit(solution)/shard_map/all_to_all | solution.py:50
  234.0 5.1 %collective-permute-done.33 = f32[4,48,128]{2,1,0:T(8,128)S(1)} collective-permute-done((f32[4,48,128]{2,1,0:T(8,128)S(1)}, f32[4,48,128]{2,1,0:T(8,128)S(1)}, u32[]{:S(2)}, u32[]{:S(2)}) %collective-permute-start.33) | collective-permute-done | bytes 98336 | tf_op jit(solution)/shard_map/ppermute | solution.py:35
  245.7 9.6 %update.1 = f32[1536,384]{1,0:T(8,128)} custom-call(s32[2]{0:T(128)} %pad_add_fusion.at_ref, f32[1536,384]{1,0:T(8,128)} %tile_ref.3, f32[1536,128]{1,0:T(8,128)} %bitcast.147, f32[1536,128]{1,0:T(8,128)} %bitcast.144, f32[1536,128]{1,0:T(8,128)} %bitcast.149, f32[1536,128]{1,0:T(8,128)} %bitcast.148, f32[256,384]{1,0:T(8,128)} %fusion.14.f_ref, ...), custom_call_target="tpu_custom_call" | custom-call | flops 2717908992 | bytes 7864320 | tf_op jit(solution)/shard_map/update/pallas_call | solution.py:343
  (181 shorter events, 73.8 us)
Async XLA Ops:
  1.5 21.8 %collective-permute-start.1 = (f32[48,256]{0,1:T(8,128)S(1)}, f32[48,256]{0,1:T(8,128)S(1)}, u32[]{:S(2)}, u32[]{:S(2)}) collective-permute-start(f32[48,256]{0,1:T(8,128)S(1)} %get-tuple-element.31), channel_id=1, source_target_pairs={{0,2},{1,18},{2,3},{3,19},{4,34},{5,50},{6,35},{7,51},{8,66},{9,82... | collective-permute-start | bytes 147464 | tf_op jit(solution)/shard_map/ppermute | solution.py:88
  9.0 15.5 %collective-permute-start.7 = (f32[48,256]{0,1:T(8,128)S(1)}, f32[48,256]{0,1:T(8,128)S(1)}, u32[]{:S(2)}, u32[]{:S(2)}) collective-permute-start(f32[48,256]{0,1:T(8,128)S(1)} %get-tuple-element.32), channel_id=1, source_target_pairs={{0,14},{1,30},{2,15},{3,31},{4,46},{5,62},{6,47},{7,63},{8,78},{9,... | collective-permute-start | bytes 147464 | tf_op jit(solution)/shard_map/ppermute | solution.py:88
  27.3 12.9 %collective-permute-start = (f32[48,256]{0,1:T(8,128)S(1)}, f32[48,256]{0,1:T(8,128)S(1)}, u32[]{:S(2)}, u32[]{:S(2)}) collective-permute-start(f32[48,256]{0,1:T(8,128)S(1)} %get-tuple-element.38), channel_id=1, source_target_pairs={{0,0},{1,16},{2,1},{3,17},{4,32},{5,48},{6,33},{7,49},{8,64},{9,80... | collective-permute-start | bytes 147464 | tf_op jit(solution)/shard_map/ppermute | solution.py:88
  40.2 18.1 %collective-permute-start.16 = (f32[48,128]{0,1:T(8,128)S(1)}, f32[48,128]{0,1:T(8,128)S(1)}, u32[]{:S(2)}, u32[]{:S(2)}) collective-permute-start(f32[48,128]{0,1:T(8,128)S(1)} %get-tuple-element.41), channel_id=1, source_target_pairs={{0,4},{2,6},{4,0},{6,2},{1,5},{3,7},{5,1},{7,3},{8,12},{10,14},{12... | collective-permute-start | bytes 73736 | tf_op jit(solution)/shard_map/ppermute | solution.py:35
  42.4 16.1 %collective-permute-start.15 = (f32[48,128]{0,1:T(8,128)S(1)}, f32[48,128]{0,1:T(8,128)S(1)}, u32[]{:S(2)}, u32[]{:S(2)}) collective-permute-start(f32[48,128]{0,1:T(8,128)S(1)} %get-tuple-element.41), channel_id=1, source_target_pairs={{0,2},{2,4},{4,6},{6,0},{1,3},{3,5},{5,7},{7,1},{8,10},{10,12},{12... | collective-permute-start | bytes 73736 | tf_op jit(solution)/shard_map/ppermute | solution.py:35
  56.9 20.0 %collective-permute-start.13 = (f32[4,48,128]{2,1,0:T(8,128)S(1)}, f32[4,48,128]{2,1,0:T(8,128)S(1)}, u32[]{:S(2)}, u32[]{:S(2)}) collective-permute-start(f32[4,48,128]{2,1,0:T(8,128)S(1)} %constant_dynamic-update-slice_fusion.8), channel_id=1, source_target_pairs={{0,6},{2,0},{4,2},{6,4},{1,7},{3,1},{5,3},{7,5},{8,14},{10,8},{12,... | collective-permute-start | bytes 294920 | tf_op jit(solution)/shard_map/ppermute | solution.py:35
  56.9 19.8 %collective-permute-start.12 = (f32[4,48,128]{2,1,0:T(8,128)S(1)}, f32[4,48,128]{2,1,0:T(8,128)S(1)}, u32[]{:S(2)}, u32[]{:S(2)}) collective-permute-start(f32[4,48,128]{2,1,0:T(8,128)S(1)} %constant_dynamic-update-slice_fusion.8), channel_id=1, source_target_pairs={{0,4},{2,6},{4,0},{6,2},{1,5},{3,7},{5,1},{7,3},{8,12},{10,14},{12... | collective-permute-start | bytes 294920 | tf_op jit(solution)/shard_map/ppermute | solution.py:35
  58.3 18.4 %collective-permute-start.11 = (f32[4,48,128]{2,1,0:T(8,128)S(1)}, f32[4,48,128]{2,1,0:T(8,128)S(1)}, u32[]{:S(2)}, u32[]{:S(2)}) collective-permute-start(f32[4,48,128]{2,1,0:T(8,128)S(1)} %constant_dynamic-update-slice_fusion.8), channel_id=1, source_target_pairs={{0,2},{2,4},{4,6},{6,0},{1,3},{3,5},{5,7},{7,1},{8,10},{10,12},{12... | collective-permute-start | bytes 294920 | tf_op jit(solution)/shard_map/ppermute | solution.py:35
  58.8 12.6 %collective-permute-start.20 = (f32[4,48,128]{2,1,0:T(8,128)S(1)}, f32[4,48,128]{2,1,0:T(8,128)S(1)}, u32[]{:S(2)}, u32[]{:S(2)}) collective-permute-start(f32[4,48,128]{2,1,0:T(8,128)S(1)} %constant_dynamic-update-slice_fusion.3), channel_id=1, source_target_pairs={{0,24},{8,0},{16,8},{24,16},{1,25},{9,1},{17,9},{25,17},{2,26},{10... | collective-permute-start | bytes 294920 | tf_op jit(solution)/shard_map/ppermute | solution.py:35
  106.0 16.9 %all-to-all-start.1 = ((f32[16,16,256]{2,1,0:T(8,128)}), f32[16,16,256]{2,1,0:T(8,128)S(1)}, u32[]{:S(2)}, u32[]{:S(2)}) async-start(f32[16,16,256]{2,1,0:T(8,128)} %broadcast_in_dim.197), calls=%async_computation.1 | async-start | bytes 524288 | tf_op jit(solution)/shard_map/all_to_all | solution.py:50
  130.8 24.4 %all-to-all-start.3 = ((f32[8,48,512]{2,1,0:T(8,128)}), f32[8,48,512]{2,1,0:T(8,128)S(1)}, u32[]{:S(2)}, u32[]{:S(2)}) async-start(f32[8,48,512]{2,1,0:T(8,128)} %bitcast.33), calls=%async_computation.3 | async-start | bytes 1572864 | tf_op jit(solution)/shard_map/all_to_all | solution.py:403
  157.5 22.9 %all-to-all-start.4 = ((f32[8,48,512]{2,1,0:T(8,128)}), f32[8,48,512]{2,1,0:T(8,128)S(1)}, u32[]{:S(2)}, u32[]{:S(2)}) async-start(f32[8,48,512]{2,1,0:T(8,128)} %broadcast_in_dim.199), calls=%async_computation.4 | async-start | bytes 1572864 | tf_op jit(solution)/shard_map/all_to_all | solution.py:50
  185.7 25.5 %collective-permute-start.27 = (f32[48,128]{1,0:T(8,128)S(1)}, f32[48,128]{1,0:T(8,128)S(1)}, u32[]{:S(2)}, u32[]{:S(2)}) collective-permute-start(f32[48,128]{1,0:T(8,128)S(1)} %get-tuple-element.45), channel_id=1, source_target_pairs={{0,4},{2,6},{4,0},{6,2},{1,5},{3,7},{5,1},{7,3},{8,12},{10,14},{12... | collective-permute-start | bytes 73736 | tf_op jit(solution)/shard_map/ppermute | solution.py:35
  190.9 17.7 %collective-permute-start.26 = (f32[48,128]{1,0:T(8,128)S(1)}, f32[48,128]{1,0:T(8,128)S(1)}, u32[]{:S(2)}, u32[]{:S(2)}) collective-permute-start(f32[48,128]{1,0:T(8,128)S(1)} %get-tuple-element.45), channel_id=1, source_target_pairs={{0,2},{2,4},{4,6},{6,0},{1,3},{3,5},{5,7},{7,1},{8,10},{10,12},{12... | collective-permute-start | bytes 73736 | tf_op jit(solution)/shard_map/ppermute | solution.py:35
  192.5 18.8 %collective-permute-start.28 = (f32[48,128]{1,0:T(8,128)S(1)}, f32[48,128]{1,0:T(8,128)S(1)}, u32[]{:S(2)}, u32[]{:S(2)}) collective-permute-start(f32[48,128]{1,0:T(8,128)S(1)} %get-tuple-element.45), channel_id=1, source_target_pairs={{0,6},{2,0},{4,2},{6,4},{1,7},{3,1},{5,3},{7,5},{8,14},{10,8},{12,... | collective-permute-start | bytes 73736 | tf_op jit(solution)/shard_map/ppermute | solution.py:35
  194.2 17.2 %collective-permute-start.24 = (f32[48,128]{1,0:T(8,128)S(1)}, f32[48,128]{1,0:T(8,128)S(1)}, u32[]{:S(2)}, u32[]{:S(2)}) collective-permute-start(f32[48,128]{1,0:T(8,128)S(1)} %get-tuple-element.46), channel_id=1, source_target_pairs={{0,16},{8,24},{16,0},{24,8},{1,17},{9,25},{17,1},{25,9},{2,18},{10... | collective-permute-start | bytes 73736 | tf_op jit(solution)/shard_map/ppermute | solution.py:35
  195.4 16.0 %collective-permute-start.23 = (f32[48,128]{1,0:T(8,128)S(1)}, f32[48,128]{1,0:T(8,128)S(1)}, u32[]{:S(2)}, u32[]{:S(2)}) collective-permute-start(f32[48,128]{1,0:T(8,128)S(1)} %get-tuple-element.46), channel_id=1, source_target_pairs={{0,8},{8,16},{16,24},{24,0},{1,9},{9,17},{17,25},{25,1},{2,10},{10... | collective-permute-start | bytes 73736 | tf_op jit(solution)/shard_map/ppermute | solution.py:35
  200.4 19.4 %all-to-all-start.5 = ((f32[32,8,256]{2,1,0:T(8,128)}), f32[32,8,256]{2,1,0:T(8,128)S(1)}, u32[]{:S(2)}, u32[]{:S(2)}) async-start(f32[32,8,256]{2,1,0:T(8,128)} %convolution_bitcast_fusion), calls=%async_computation.5 | async-start | bytes 524288 | tf_op jit(solution)/shard_map/all_to_all | solution.py:417
  219.9 13.3 %collective-permute-start.31 = (f32[4,48,128]{2,1,0:T(8,128)S(1)}, f32[4,48,128]{2,1,0:T(8,128)S(1)}, u32[]{:S(2)}, u32[]{:S(2)}) collective-permute-start(f32[4,48,128]{2,1,0:T(8,128)S(1)} %bitcast_dynamic-update-slice_fusion.24), channel_id=1, source_target_pairs={{0,6},{2,0},{4,2},{6,4},{1,7},{3,1},{5,3},{7,5},{8,14},{10,8},{12,... | collective-permute-start | bytes 294920 | tf_op jit(solution)/shard_map/ppermute | solution.py:35
  221.1 12.0 %collective-permute-start.30 = (f32[4,48,128]{2,1,0:T(8,128)S(1)}, f32[4,48,128]{2,1,0:T(8,128)S(1)}, u32[]{:S(2)}, u32[]{:S(2)}) collective-permute-start(f32[4,48,128]{2,1,0:T(8,128)S(1)} %bitcast_dynamic-update-slice_fusion.24), channel_id=1, source_target_pairs={{0,4},{2,6},{4,0},{6,2},{1,5},{3,7},{5,1},{7,3},{8,12},{10,14},{12... | collective-permute-start | bytes 294920 | tf_op jit(solution)/shard_map/ppermute | solution.py:35
  221.1 10.6 %collective-permute-start.29 = (f32[4,48,128]{2,1,0:T(8,128)S(1)}, f32[4,48,128]{2,1,0:T(8,128)S(1)}, u32[]{:S(2)}, u32[]{:S(2)}) collective-permute-start(f32[4,48,128]{2,1,0:T(8,128)S(1)} %bitcast_dynamic-update-slice_fusion.24), channel_id=1, source_target_pairs={{0,2},{2,4},{4,6},{6,0},{1,3},{3,5},{5,7},{7,1},{8,10},{10,12},{12... | collective-permute-start | bytes 294920 | tf_op jit(solution)/shard_map/ppermute | solution.py:35
  221.5 17.6 %collective-permute-start.35 = (f32[4,48,128]{2,1,0:T(8,128)S(1)}, f32[4,48,128]{2,1,0:T(8,128)S(1)}, u32[]{:S(2)}, u32[]{:S(2)}) collective-permute-start(f32[4,48,128]{2,1,0:T(8,128)S(1)} %bitcast_dynamic-update-slice_fusion.20), channel_id=1, source_target_pairs={{0,24},{8,0},{16,8},{24,16},{1,25},{9,1},{17,9},{25,17},{2,26},{10... | collective-permute-start | bytes 294920 | tf_op jit(solution)/shard_map/ppermute | solution.py:35
  222.4 16.7 %collective-permute-start.34 = (f32[4,48,128]{2,1,0:T(8,128)S(1)}, f32[4,48,128]{2,1,0:T(8,128)S(1)}, u32[]{:S(2)}, u32[]{:S(2)}) collective-permute-start(f32[4,48,128]{2,1,0:T(8,128)S(1)} %bitcast_dynamic-update-slice_fusion.20), channel_id=1, source_target_pairs={{0,16},{8,24},{16,0},{24,8},{1,17},{9,25},{17,1},{25,9},{2,18},{10... | collective-permute-start | bytes 294920 | tf_op jit(solution)/shard_map/ppermute | solution.py:35
  224.4 18.5 %all-to-all-start.6 = ((f32[32,8,256]{2,1,0:T(8,128)}), f32[32,8,256]{2,1,0:T(8,128)S(1)}, u32[]{:S(2)}, u32[]{:S(2)}) async-start(f32[32,8,256]{2,1,0:T(8,128)} %broadcast_in_dim.220), calls=%async_computation.6 | async-start | bytes 524288 | tf_op jit(solution)/shard_map/all_to_all | solution.py:50
  (26 other events, 168.8 us)
where the time goes:
time: 256 us; the launch traced here: 255 us
  starting transfers between devices  109 us (43%)
  waiting for transfers between devices  58 us (23%)
  Pallas kernels  40.7 us (16%)
  blocking collectives  24.8 us (10%)
  local copies, waits for them, and re-layouts  9.61 us (4%)
  matrix products  8.5 us (3%)
  other arithmetic  3.72 us (1%)
    ppermute x28, starting transfers between devices, shifted(): lax.ppermute(value, axis, [(k, (k + by) % size) for k in range(size)])  47.1 us
    ppermute x8, starting transfers between devices, spread_strip(): got = lax.ppermute(parts[r], ALL, moves)  27.6 us
    pallas_call x2, Pallas kernels, on_squares(): pl.pallas_call(kernel, out_shape=(square,) * outputs, in_specs=[vmem] * l...  25.9 us
    ppermute x28, waiting for transfers between devices, shifted(): lax.ppermute(value, axis, [(k, (k + by) % size) for k in range(size)])  19.6 us
    all_to_all x3, starting transfers between devices, from_everyone(): lax.all_to_all(jnp.broadcast_to(value[None], (size, *value.shape)), axis,...  19 us
    all_to_all x1, blocking collectives, per_device(): message = lax.all_to_all(message, ROW, 0, 0, tiled=True)  17.8 us
    ppermute x8, waiting for transfers between devices, spread_strip(): got = lax.ppermute(parts[r], ALL, moves)  10.8 us
    pallas_call x1, Pallas kernels, updated(): pl.pallas_call(update_kernel, out_shape=jax.ShapeDtypeStruct(tile.shape,...  9.56 us
  transfers between devices with their start and end apart: 42, of which 16 were waited for; matrix products, arithmetic and copies ran while one was open for 4% of the time, Pallas kernels for 10%

commit v1 on v0

--- a/solution.py
+++ b/solution.py
@@ -18,6 +18,7 @@
 HIGHEST = lax.Precision.HIGHEST
 INTERPRET = False
 STEP = 64
+LINES = 768
 
 
 def contract(left_op, right_op, left_dim, right_dim, precision=HIGHEST):
@@ -79,6 +80,7 @@
 TO_PLANE = [
     (r * 32 + j, (j // 4) * 32 + plane_place((j % 4) * 8 + r)) for r in range(8) for j in range(32)
 ]
+TO_ROWS = [(there, here) for here, there in TO_PLANE]
 
 
 def spread_strip(parts):
@@ -259,7 +261,7 @@
 
 def products(tile, left, right):
     rows_dev, cols_dev = tile.shape
-    lines = 2 * B
+    lines = LINES
     return pl.pallas_call(
         products_kernel,
         out_shape=(
@@ -303,32 +305,30 @@
     both = jnp.concatenate([lefts(panel, 3, 1), lefts(u_mat, 2, 1)], axis=1)
     out_ref[...] = tile_ref[...] - dot(both, factors[...], 1, 0)
 
-    @pl.when((row_at == 0) & (step == 1))
-    def _():
-        out_ref[...] = out_ref[...] + w_ref[...]
-
     top = (row_at == 0) & (step == 0)
 
+    @pl.when(top)
+    def _():
+        out_ref[B : 2 * B, :] = out_ref[B : 2 * B, :] + w_ref[...]
+
     @pl.when((col_at == 0) & jnp.logical_not(top))
     def _():
-        out_ref[:, :B] = jnp.zeros((B, B), jnp.float32)
-
-    @pl.when((col_at == 0) & (row_at == 0) & (step == 1))
-    def _():
-        out_ref[:, :B] = r_ref[...]
-
-    @pl.when(top & (col_at == 0))
-    def _():
-        out_ref[:, B:] = rt_ref[:, : B // 2]
-
-    @pl.when(top & (col_at == 1))
-    def _():
-        out_ref[:, : B // 2] = rt_ref[:, B // 2 :]
-        out_ref[:, B // 2 :] = jnp.zeros((B, B), jnp.float32)
-
-    @pl.when(top & (col_at >= 2))
-    def _():
-        out_ref[...] = jnp.zeros(out_ref.shape, jnp.float32)
+        out_ref[:, :B] = jnp.zeros((LINES, B), jnp.float32)
+
+    @pl.when((col_at == 0) & top)
+    def _():
+        out_ref[B : 2 * B, :B] = r_ref[...]
+        out_ref[2 * B :, :B] = jnp.zeros((LINES - 2 * B, B), jnp.float32)
+        out_ref[:B, B:] = rt_ref[:, : B // 2]
+
+    @pl.when((col_at == 1) & top)
+    def _():
+        out_ref[:B, : B // 2] = rt_ref[:, B // 2 :]
+        out_ref[:B, B // 2 :] = jnp.zeros((B, B), jnp.float32)
+
+    @pl.when((col_at >= 2) & top)
+    def _():
+        out_ref[:B, :] = jnp.zeros((B, out_ref.shape[1]), jnp.float32)
 
 
 def updated(at, tile, panel, u_mat, small, upper):
@@ -338,14 +338,14 @@
         return pl.BlockSpec(shape, lambda k, at: (0, 0))
 
     def lines(width):
-        return pl.BlockSpec((B, width), lambda k, at: (k, 0))
+        return pl.BlockSpec((LINES, width), lambda k, at: (k, 0))
 
     return pl.pallas_call(
         update_kernel,
         out_shape=jax.ShapeDtypeStruct(tile.shape, jnp.float32),
         grid_spec=pltpu.PrefetchScalarGridSpec(
             num_scalar_prefetch=1,
-            grid=(rows_dev // B,),
+            grid=(rows_dev // LINES,),
             in_specs=[lines(cols_dev)]
             + [lines(B // 2)] * 4
             + [whole((B, cols_dev))] * 3
@@ -380,6 +380,8 @@
     panel_part = spread_strip(strip.reshape(8, -1, B))
     panel = plane_gather(panel_part)
 
+    panel_part, *panel = lax.optimization_barrier((panel_part, *panel))
+    panel_there = lax.ppermute(panel_part, ALL, TO_ROWS)
     gram, product = products(tile, *panel)
     gram_slice = lax.dynamic_slice_in_dim(gram, place * 8, 8, 0)
     lead_slice = jnp.concatenate(
@@ -398,15 +400,15 @@
     gram = message[:, 0].reshape(B, B)
     lead = message[:, 1].reshape(B, B)
 
-    both = jnp.concatenate([strip, tile[B : 2 * B, :].T], axis=1).reshape(8, -1, 2 * B)
-    both, gram = lax.optimization_barrier((both, gram))
-    both = lax.all_to_all(both, ROW, 0, 0, tiled=True)
-    both = both.reshape(8, -1, 2 * B)[0]
+    edge = tile[B : 2 * B, :].T.reshape(8, -1, B)
+    edge, gram = lax.optimization_barrier((edge, gram))
+    edge = lax.all_to_all(edge, ROW, 0, 0, tiled=True)
+    edge = edge.reshape(8, -1, B)[0]
     upper, inverse = chol(gram)
 
-    u_part = contract(product_part, inverse, 1, 1) - both[:, B:]
+    u_part = contract(product_part, inverse, 1, 1) - edge
     u_there = lax.ppermute(u_part, ALL, TO_PLANE)
-    both_j = row_gather(jnp.concatenate([both[:, :B], u_part], axis=1))
+    both_j = row_gather(jnp.concatenate([panel_there, u_part], axis=1))
     t_mat = t_inverse(lead, inverse)
     unit_j = (global_cols[:, None] - B == band[None, :]).astype(jnp.float32)
     reflector_j = contract(both_j[:, :B], inverse, 1, 1) - unit_j

time: 256 us -> 242 us (0.945)
  waiting for transfers between devices: 58 us -> 43.7 us
  local copies, waits for them, and re-layouts: 9.61 us -> 12.3 us
    all_to_all x1, waiting for transfers between devices: 8.42 us -> 0.01 us  [per_device(): edge = lax.all_to_all(edge, ROW, 0, 0, tiled=True)]
    ppermute x8, waiting for transfers between devices: 10.8 us -> 3.26 us  [spread_strip(): got = lax.ppermute(parts[r], ALL, moves)]
    all_to_all x3, starting transfers between devices: 19 us -> 25.9 us  [from_everyone(): lax.all_to_all(jnp.broadcast_to(value[None], (size, *value.shape)), axis,...]
    ppermute x28, starting transfers between devices: 47.1 us -> 41.7 us  [shifted(): lax.ppermute(value, axis, [(k, (k + by) % size) for k in range(size)])]
    ppermute x28, waiting for transfers between devices: 19.6 us -> 23.1 us  [shifted(): lax.ppermute(value, axis, [(k, (k + by) % size) for k in range(size)])]
  transfers between devices with their start and end apart: 42 -> 43, of which waited for: 16 -> 12; matrix products, arithmetic and copies ran while one was open for 4% -> 5% of each run, Pallas kernels for 10% -> 11%
where the time goes in v1:
time: 242 us; the launch traced here: 241 us
  starting transfers between devices  110 us (45%)
  waiting for transfers between devices  43.7 us (18%)
  Pallas kernels  39.3 us (16%)
  blocking collectives  23.3 us (10%)
  local copies, waits for them, and re-layouts  12.3 us (5%)
  matrix products  8.53 us (4%)
  other arithmetic  2.59 us (1%)
    ppermute x28, starting transfers between devices, shifted(): lax.ppermute(value, axis, [(k, (k + by) % size) for k in range(size)])  41.7 us
    ppermute x8, starting transfers between devices, spread_strip(): got = lax.ppermute(parts[r], ALL, moves)  26.4 us
    all_to_all x3, starting transfers between devices, from_everyone(): lax.all_to_all(jnp.broadcast_to(value[None], (size, *value.shape)), axis,...  25.9 us
    pallas_call x2, Pallas kernels, on_squares(): pl.pallas_call(kernel, out_shape=(square,) * outputs, in_specs=[vmem] * l...  25.9 us
    ppermute x28, waiting for transfers between devices, shifted(): lax.ppermute(value, axis, [(k, (k + by) % size) for k in range(size)])  23.1 us
    all_to_all x1, blocking collectives, per_device(): message = lax.all_to_all(message, ROW, 0, 0, tiled=True)  17.6 us
    all_to_all x3, waiting for transfers between devices, from_everyone(): lax.all_to_all(jnp.broadcast_to(value[None], (size, *value.shape)), axis,...  9.01 us
    dot_general x9, matrix products, contract(): lax.dot_general(left_op, right_op, (((left_dim,), (right_dim,)), ((), ())...  8.53 us
  transfers between devices with their start and end apart: 43, of which 12 were waited for; matrix products, arithmetic and copies ran while one was open for 5% of the time, Pallas kernels for 11%

profile of v1, /device:TPU:1, one launch (start us, length us, event | category | flops | bytes accessed | tf_op | source)
XLA Modules:
  0.0 241.1 jit_solution(3034940631914816602)
XLA Ops:
  1.5 7.6 %collective-permute-start.1 = (f32[48,256]{1,0:T(8,128)S(1)}, f32[48,256]{1,0:T(8,128)S(1)}, u32[]{:S(2)}, u32[]{:S(2)}) collective-permute-start(f32[48,256]{1,0:T(8,128)S(1)} %get-tuple-element.37), channel_id=1, source_target_pairs={{0,2},{1,18},{2,3},{3,19},{4,34},{5,50},{6,35},{7,51},{8,66},{9,82... | collective-permute-start | bytes 147464 | tf_op jit(solution)/shard_map/ppermute | solution.py:90
  9.1 9.3 %collective-permute-start.7 = (f32[48,256]{1,0:T(8,128)S(1)}, f32[48,256]{1,0:T(8,128)S(1)}, u32[]{:S(2)}, u32[]{:S(2)}) collective-permute-start(f32[48,256]{1,0:T(8,128)S(1)} %get-tuple-element.38), channel_id=1, source_target_pairs={{0,14},{1,30},{2,15},{3,31},{4,46},{5,62},{6,47},{7,63},{8,78},{9,... | collective-permute-start | bytes 147464 | tf_op jit(solution)/shard_map/ppermute | solution.py:90
  28.2 3.2 %collective-permute-done = f32[48,256]{1,0:T(8,128)S(1)} collective-permute-done((f32[48,256]{1,0:T(8,128)S(1)}, f32[48,256]{1,0:T(8,128)S(1)}, u32[]{:S(2)}, u32[]{:S(2)}) %collective-permute-start) | collective-permute-done | bytes 49184 | tf_op jit(solution)/shard_map/ppermute | solution.py:90
  31.7 3.3 %collective-permute-start.17 = (f32[48,128]{1,0:T(8,128)S(1)}, f32[48,128]{1,0:T(8,128)S(1)}, u32[]{:S(2)}, u32[]{:S(2)}) collective-permute-start(f32[48,128]{1,0:T(8,128)S(1)} %get-tuple-element.49), channel_id=1, source_target_pairs={{0,6},{2,0},{4,2},{6,4},{1,7},{3,1},{5,3},{7,5},{8,14},{10,8},{12,... | collective-permute-start | bytes 73736 | tf_op jit(solution)/shard_map/ppermute | solution.py:36
  36.3 3.8 %collective-permute-done.8 = f32[48,128]{1,0:T(8,128)S(1)} collective-permute-done((f32[48,128]{1,0:T(8,128)S(1)}, f32[48,128]{1,0:T(8,128)S(1)}, u32[]{:S(2)}, u32[]{:S(2)}) %collective-permute-start.8) | collective-permute-done | bytes 24608 | tf_op jit(solution)/shard_map/ppermute | solution.py:36
  46.5 4.7 %collective-permute-done.18 = f32[4,48,128]{2,1,0:T(8,128)S(1)} collective-permute-done((f32[4,48,128]{2,1,0:T(8,128)S(1)}, f32[4,48,128]{2,1,0:T(8,128)S(1)}, u32[]{:S(2)}, u32[]{:S(2)}) %collective-permute-start.18) | collective-permute-done | bytes 98336 | tf_op jit(solution)/shard_map/ppermute | solution.py:36
  51.2 5.1 %collective-permute-done.19 = f32[4,48,128]{2,1,0:T(8,128)S(1)} collective-permute-done((f32[4,48,128]{2,1,0:T(8,128)S(1)}, f32[4,48,128]{2,1,0:T(8,128)S(1)}, u32[]{:S(2)}, u32[]{:S(2)}) %collective-permute-start.19) | collective-permute-done | bytes 98336 | tf_op jit(solution)/shard_map/ppermute | solution.py:36
  56.3 7.8 %collective-permute-start.21 = (f32[768,128]{1,0:T(8,128)S(1)}, f32[768,128]{1,0:T(8,128)S(1)}, u32[]{:S(2)}, u32[]{:S(2)}) collective-permute-start(f32[768,128]{1,0:T(8,128)S(1)} %bitcast.146), channel_id=1, source_target_pairs={{0,1},{1,0},{2,3},{3,2},{4,5},{5,4},{6,7},{7,6},{8,9},{9,8},{10,11... | collective-permute-start | bytes 1179656 | tf_op jit(solution)/shard_map/ppermute | solution.py:36
  67.1 4.9 %products.1 = (f32[256,256]{1,0:T(8,128)}, f32[384,256]{1,0:T(8,128)}) custom-call(f32[1536,384]{1,0:T(8,128)} %tile_ref.3, f32[1536,128]{1,0:T(8,128)} %bitcast.150, f32[1536,128]{1,0:T(8,128)} %bitcast.153), custom_call_target="tpu_custom_call" | custom-call | flops 2113929216 | bytes 3932160 | tf_op jit(solution)/shard_map/products/pallas_call | solution.py:265
  74.5 17.6 %all_to_all.36 = f32[8,64,256]{2,1,0:T(8,128)S(1)} all-to-all(f32[8,64,256]{2,1,0:T(8,128)S(1)} %pad_maximum_fusion), channel_id=1, replica_groups=mesh['x'=4,'zh'=2,'y'=4,'zl'=4,'c'=2] {'x','zh'}, dimensions={0} | all-to-all | bytes 1048576 | tf_op jit(solution)/shard_map/all_to_all | solution.py:395
  92.9 9.8 %all-to-all-start.1 = ((f32[16,16,256]{2,1,0:T(8,128)}), f32[16,16,256]{2,1,0:T(8,128)S(1)}, u32[]{:S(2)}, u32[]{:S(2)}) async-start(f32[16,16,256]{2,1,0:T(8,128)} %broadcast_in_dim.197), calls=%async_computation.1 | async-start | bytes 524288 | tf_op jit(solution)/shard_map/all_to_all | solution.py:51
  103.6 9.0 %all-to-all-done.1 = f32[16,16,256]{2,1,0:T(8,128)S(1)} async-done(((f32[16,16,256]{2,1,0:T(8,128)}), f32[16,16,256]{2,1,0:T(8,128)S(1)}, u32[]{:S(2)}, u32[]{:S(2)}) %all-to-all-start.1) | async-done | bytes 262176 | tf_op jit(solution)/shard_map/all_to_all | solution.py:51
  112.7 5.7 %all_to_all.35 = f32[2,16,16,256]{3,2,1,0:T(8,128)S(1)} all-to-all(f32[2,16,16,256]{3,2,1,0:T(8,128)S(1)} %broadcast_in_dim.198), channel_id=1, replica_groups=mesh['x'=4,'zh'=2,'y'=4,'zl'=4,'c'=2] {'c'}, dimensions={0} | all-to-all | bytes 1048576 | tf_op jit(solution)/shard_map/all_to_all | solution.py:51
  119.2 3.5 %all-to-all-start.3 = ((f32[8,48,256]{2,1,0:T(8,128)}), f32[8,48,256]{2,1,0:T(8,128)S(1)}, u32[]{:S(2)}, u32[]{:S(2)}) async-start(f32[8,48,256]{2,1,0:T(8,128)} %bitcast.33), calls=%async_computation.3 | async-start | bytes 786432 | tf_op jit(solution)/shard_map/all_to_all | solution.py:405
  124.8 12.4 %shard_map.17 = (f32[256,256]{1,0:T(8,128)}, f32[256,256]{1,0:T(8,128)}) custom-call(f32[256,256]{1,0:T(8,128)} %get-tuple-element.23.gram_ref), custom_call_target="tpu_custom_call" | custom-call | flops 2000000000 | bytes 1048576 | tf_op jit(solution)/shard_map/pallas_call | solution.py:202
  139.5 8.8 %all-to-all-start.4 = ((f32[8,48,512]{2,1,0:T(8,128)}), f32[8,48,512]{2,1,0:T(8,128)S(1)}, u32[]{:S(2)}, u32[]{:S(2)}) async-start(f32[8,48,512]{2,1,0:T(8,128)} %broadcast_in_dim.199), calls=%async_computation.4 | async-start | bytes 1572864 | tf_op jit(solution)/shard_map/all_to_all | solution.py:51
  150.6 13.5 %shard_map.18 = f32[256,256]{1,0:T(8,128)} custom-call(f32[256,256]{1,0:T(8,128)} %get-tuple-element.35.lead_ref, f32[256,256]{1,0:T(8,128)} %get-tuple-element.24.inverse_ref), custom_call_target="tpu_custom_call" | custom-call | flops 2000000000 | bytes 1048576 | tf_op jit(solution)/shard_map/pallas_call | solution.py:202
  164.1 3.4 %collective-permute-start.22 = (f32[48,256]{1,0:T(8,128)S(1)}, f32[48,256]{1,0:T(8,128)S(1)}, u32[]{:S(2)}, u32[]{:S(2)}) collective-permute-start(f32[48,256]{1,0:T(8,128)S(1)} %convolution_subtract_fusion.2), channel_id=1, source_target_pairs={{0,0},{1,16},{2,1},{3,17},{4,32},{5,48},{6,33},{7,49},{8,64},{9,80... | collective-permute-start | bytes 147464 | tf_op jit(solution)/shard_map/ppermute | solution.py:410
  170.4 7.0 %collective-permute-start.28 = (f32[48,128]{1,0:T(8,128)S(1)}, f32[48,128]{1,0:T(8,128)S(1)}, u32[]{:S(2)}, u32[]{:S(2)}) collective-permute-start(f32[48,128]{1,0:T(8,128)S(1)} %get-tuple-element.47), channel_id=1, source_target_pairs={{0,4},{2,6},{4,0},{6,2},{1,5},{3,7},{5,1},{7,3},{8,12},{10,14},{12... | collective-permute-start | bytes 73736 | tf_op jit(solution)/shard_map/ppermute | solution.py:36
  187.7 7.3 %all-to-all-start.5 = ((f32[32,8,256]{2,1,0:T(8,128)}), f32[32,8,256]{2,1,0:T(8,128)S(1)}, u32[]{:S(2)}, u32[]{:S(2)}) async-start(f32[32,8,256]{2,1,0:T(8,128)} %convolution_bitcast_fusion), calls=%async_computation.5 | async-start | bytes 524288 | tf_op jit(solution)/shard_map/all_to_all | solution.py:419
  198.7 7.6 %all-to-all-done.5 = f32[32,8,256]{2,1,0:T(8,128)S(1)} async-done(((f32[32,8,256]{2,1,0:T(8,128)}), f32[32,8,256]{2,1,0:T(8,128)S(1)}, u32[]{:S(2)}, u32[]{:S(2)}) %all-to-all-start.5) | async-done | bytes 262176 | tf_op jit(solution)/shard_map/all_to_all | solution.py:419
  210.3 7.4 %all-to-all-start.6 = ((f32[32,8,256]{2,1,0:T(8,128)}), f32[32,8,256]{2,1,0:T(8,128)S(1)}, u32[]{:S(2)}, u32[]{:S(2)}) async-start(f32[32,8,256]{2,1,0:T(8,128)} %broadcast_in_dim.220), calls=%async_computation.6 | async-start | bytes 524288 | tf_op jit(solution)/shard_map/all_to_all | solution.py:51
  220.6 4.5 %collective-permute-done.35 = f32[4,48,128]{2,1,0:T(8,128)S(1)} collective-permute-done((f32[4,48,128]{2,1,0:T(8,128)S(1)}, f32[4,48,128]{2,1,0:T(8,128)S(1)}, u32[]{:S(2)}, u32[]{:S(2)}) %collective-permute-start.35) | collective-permute-done | bytes 98336 | tf_op jit(solution)/shard_map/ppermute | solution.py:36
  232.6 8.5 %update.1 = f32[1536,384]{1,0:T(8,128)} custom-call(s32[2]{0:T(128)} %pad_add_fusion.at_ref, f32[1536,384]{1,0:T(8,128)} %tile_ref.3, f32[1536,128]{1,0:T(8,128)} %bitcast.152, f32[1536,128]{1,0:T(8,128)} %bitcast.155, f32[1536,128]{1,0:T(8,128)} %bitcast.58.ul_ref, f32[1536,128]{1,0:T(8,128)} %bitcast.156, f32[256,384]{1,0:T(8,128)} %fusion.14.f_ref, ...), custom_call_target="tpu_custom_call" | custom-call | flops 2717908992 | bytes 7864320 | tf_op jit(solution)/shard_map/update/pallas_call | solution.py:343
  (172 shorter events, 64.5 us)
Async XLA Ops:
  1.5 21.7 %collective-permute-start.1 = (f32[48,256]{1,0:T(8,128)S(1)}, f32[48,256]{1,0:T(8,128)S(1)}, u32[]{:S(2)}, u32[]{:S(2)}) collective-permute-start(f32[48,256]{1,0:T(8,128)S(1)} %get-tuple-element.37), channel_id=1, source_target_pairs={{0,2},{1,18},{2,3},{3,19},{4,34},{5,50},{6,35},{7,51},{8,66},{9,82... | collective-permute-start | bytes 147464 | tf_op jit(solution)/shard_map/ppermute | solution.py:90
  9.1 15.5 %collective-permute-start.7 = (f32[48,256]{1,0:T(8,128)S(1)}, f32[48,256]{1,0:T(8,128)S(1)}, u32[]{:S(2)}, u32[]{:S(2)}) collective-permute-start(f32[48,256]{1,0:T(8,128)S(1)} %get-tuple-element.38), channel_id=1, source_target_pairs={{0,14},{1,30},{2,15},{3,31},{4,46},{5,62},{6,47},{7,63},{8,78},{9,... | collective-permute-start | bytes 147464 | tf_op jit(solution)/shard_map/ppermute | solution.py:90
  31.5 13.1 %collective-permute-start.16 = (f32[48,128]{1,0:T(8,128)S(1)}, f32[48,128]{1,0:T(8,128)S(1)}, u32[]{:S(2)}, u32[]{:S(2)}) collective-permute-start(f32[48,128]{1,0:T(8,128)S(1)} %get-tuple-element.49), channel_id=1, source_target_pairs={{0,4},{2,6},{4,0},{6,2},{1,5},{3,7},{5,1},{7,3},{8,12},{10,14},{12... | collective-permute-start | bytes 73736 | tf_op jit(solution)/shard_map/ppermute | solution.py:36
  31.6 11.5 %collective-permute-start.15 = (f32[48,128]{1,0:T(8,128)S(1)}, f32[48,128]{1,0:T(8,128)S(1)}, u32[]{:S(2)}, u32[]{:S(2)}) collective-permute-start(f32[48,128]{1,0:T(8,128)S(1)} %get-tuple-element.49), channel_id=1, source_target_pairs={{0,2},{2,4},{4,6},{6,0},{1,3},{3,5},{5,7},{7,1},{8,10},{10,12},{12... | collective-permute-start | bytes 73736 | tf_op jit(solution)/shard_map/ppermute | solution.py:36
  31.7 12.9 %collective-permute-start.17 = (f32[48,128]{1,0:T(8,128)S(1)}, f32[48,128]{1,0:T(8,128)S(1)}, u32[]{:S(2)}, u32[]{:S(2)}) collective-permute-start(f32[48,128]{1,0:T(8,128)S(1)} %get-tuple-element.49), channel_id=1, source_target_pairs={{0,6},{2,0},{4,2},{6,4},{1,7},{3,1},{5,3},{7,5},{8,14},{10,8},{12,... | collective-permute-start | bytes 73736 | tf_op jit(solution)/shard_map/ppermute | solution.py:36
  42.8 21.4 %collective-permute-start.13 = (f32[4,48,128]{2,1,0:T(8,128)S(1)}, f32[4,48,128]{2,1,0:T(8,128)S(1)}, u32[]{:S(2)}, u32[]{:S(2)}) collective-permute-start(f32[4,48,128]{2,1,0:T(8,128)S(1)} %bitcast_dynamic-update-slice_fusion.32), channel_id=1, source_target_pairs={{0,6},{2,0},{4,2},{6,4},{1,7},{3,1},{5,3},{7,5},{8,14},{10,8},{12,... | collective-permute-start | bytes 294920 | tf_op jit(solution)/shard_map/ppermute | solution.py:36
  42.8 21.3 %collective-permute-start.12 = (f32[4,48,128]{2,1,0:T(8,128)S(1)}, f32[4,48,128]{2,1,0:T(8,128)S(1)}, u32[]{:S(2)}, u32[]{:S(2)}) collective-permute-start(f32[4,48,128]{2,1,0:T(8,128)S(1)} %bitcast_dynamic-update-slice_fusion.32), channel_id=1, source_target_pairs={{0,4},{2,6},{4,0},{6,2},{1,5},{3,7},{5,1},{7,3},{8,12},{10,14},{12... | collective-permute-start | bytes 294920 | tf_op jit(solution)/shard_map/ppermute | solution.py:36
  43.1 21.0 %collective-permute-start.11 = (f32[4,48,128]{2,1,0:T(8,128)S(1)}, f32[4,48,128]{2,1,0:T(8,128)S(1)}, u32[]{:S(2)}, u32[]{:S(2)}) collective-permute-start(f32[4,48,128]{2,1,0:T(8,128)S(1)} %bitcast_dynamic-update-slice_fusion.32), channel_id=1, source_target_pairs={{0,2},{2,4},{4,6},{6,0},{1,3},{3,5},{5,7},{7,1},{8,10},{10,12},{12... | collective-permute-start | bytes 294920 | tf_op jit(solution)/shard_map/ppermute | solution.py:36
  44.6 11.7 %collective-permute-start.20 = (f32[4,48,128]{2,1,0:T(8,128)S(1)}, f32[4,48,128]{2,1,0:T(8,128)S(1)}, u32[]{:S(2)}, u32[]{:S(2)}) collective-permute-start(f32[4,48,128]{2,1,0:T(8,128)S(1)} %bitcast_dynamic-update-slice_fusion.28), channel_id=1, source_target_pairs={{0,24},{8,0},{16,8},{24,16},{1,25},{9,1},{17,9},{25,17},{2,26},{10... | collective-permute-start | bytes 294920 | tf_op jit(solution)/shard_map/ppermute | solution.py:36
  92.9 19.7 %all-to-all-start.1 = ((f32[16,16,256]{2,1,0:T(8,128)}), f32[16,16,256]{2,1,0:T(8,128)S(1)}, u32[]{:S(2)}, u32[]{:S(2)}) async-start(f32[16,16,256]{2,1,0:T(8,128)} %broadcast_in_dim.197), calls=%async_computation.1 | async-start | bytes 524288 | tf_op jit(solution)/shard_map/all_to_all | solution.py:51
  119.2 18.0 %all-to-all-start.3 = ((f32[8,48,256]{2,1,0:T(8,128)}), f32[8,48,256]{2,1,0:T(8,128)S(1)}, u32[]{:S(2)}, u32[]{:S(2)}) async-start(f32[8,48,256]{2,1,0:T(8,128)} %bitcast.33), calls=%async_computation.3 | async-start | bytes 786432 | tf_op jit(solution)/shard_map/all_to_all | solution.py:405
  122.7 15.9 %collective-permute-start.23 = (f32[48,256]{1,0:T(8,128)S(1)}, f32[48,256]{1,0:T(8,128)S(1)}, u32[]{:S(2)}, u32[]{:S(2)}) collective-permute-start(f32[48,256]{1,0:T(8,128)S(1)} %add_add_fusion), channel_id=1, source_target_pairs={{0,0},{16,1},{1,2},{17,3},{32,4},{48,5},{33,6},{49,7},{64,8},{80,9... | collective-permute-start | bytes 147464 | tf_op jit(solution)/shard_map/ppermute | solution.py:384
  139.5 28.0 %all-to-all-start.4 = ((f32[8,48,512]{2,1,0:T(8,128)}), f32[8,48,512]{2,1,0:T(8,128)S(1)}, u32[]{:S(2)}, u32[]{:S(2)}) async-start(f32[8,48,512]{2,1,0:T(8,128)} %broadcast_in_dim.199), calls=%async_computation.4 | async-start | bytes 1572864 | tf_op jit(solution)/shard_map/all_to_all | solution.py:51
  170.4 27.4 %collective-permute-start.28 = (f32[48,128]{1,0:T(8,128)S(1)}, f32[48,128]{1,0:T(8,128)S(1)}, u32[]{:S(2)}, u32[]{:S(2)}) collective-permute-start(f32[48,128]{1,0:T(8,128)S(1)} %get-tuple-element.47), channel_id=1, source_target_pairs={{0,4},{2,6},{4,0},{6,2},{1,5},{3,7},{5,1},{7,3},{8,12},{10,14},{12... | collective-permute-start | bytes 73736 | tf_op jit(solution)/shard_map/ppermute | solution.py:36
  177.4 17.7 %collective-permute-start.27 = (f32[48,128]{1,0:T(8,128)S(1)}, f32[48,128]{1,0:T(8,128)S(1)}, u32[]{:S(2)}, u32[]{:S(2)}) collective-permute-start(f32[48,128]{1,0:T(8,128)S(1)} %get-tuple-element.47), channel_id=1, source_target_pairs={{0,2},{2,4},{4,6},{6,0},{1,3},{3,5},{5,7},{7,1},{8,10},{10,12},{12... | collective-permute-start | bytes 73736 | tf_op jit(solution)/shard_map/ppermute | solution.py:36
  178.1 19.7 %collective-permute-start.29 = (f32[48,128]{1,0:T(8,128)S(1)}, f32[48,128]{1,0:T(8,128)S(1)}, u32[]{:S(2)}, u32[]{:S(2)}) collective-permute-start(f32[48,128]{1,0:T(8,128)S(1)} %get-tuple-element.47), channel_id=1, source_target_pairs={{0,6},{2,0},{4,2},{6,4},{1,7},{3,1},{5,3},{7,5},{8,14},{10,8},{12,... | collective-permute-start | bytes 73736 | tf_op jit(solution)/shard_map/ppermute | solution.py:36
  180.7 17.2 %collective-permute-start.25 = (f32[48,128]{1,0:T(8,128)S(1)}, f32[48,128]{1,0:T(8,128)S(1)}, u32[]{:S(2)}, u32[]{:S(2)}) collective-permute-start(f32[48,128]{1,0:T(8,128)S(1)} %get-tuple-element.48), channel_id=1, source_target_pairs={{0,16},{8,24},{16,0},{24,8},{1,17},{9,25},{17,1},{25,9},{2,18},{10... | collective-permute-start | bytes 73736 | tf_op jit(solution)/shard_map/ppermute | solution.py:36
  182.3 15.6 %collective-permute-start.24 = (f32[48,128]{1,0:T(8,128)S(1)}, f32[48,128]{1,0:T(8,128)S(1)}, u32[]{:S(2)}, u32[]{:S(2)}) collective-permute-start(f32[48,128]{1,0:T(8,128)S(1)} %get-tuple-element.48), channel_id=1, source_target_pairs={{0,8},{8,16},{16,24},{24,0},{1,9},{9,17},{17,25},{25,1},{2,10},{10... | collective-permute-start | bytes 73736 | tf_op jit(solution)/shard_map/ppermute | solution.py:36
  187.7 18.6 %all-to-all-start.5 = ((f32[32,8,256]{2,1,0:T(8,128)}), f32[32,8,256]{2,1,0:T(8,128)S(1)}, u32[]{:S(2)}, u32[]{:S(2)}) async-start(f32[32,8,256]{2,1,0:T(8,128)} %convolution_bitcast_fusion), calls=%async_computation.5 | async-start | bytes 524288 | tf_op jit(solution)/shard_map/all_to_all | solution.py:419
  206.4 20.2 %collective-permute-start.32 = (f32[4,48,128]{2,1,0:T(8,128)S(1)}, f32[4,48,128]{2,1,0:T(8,128)S(1)}, u32[]{:S(2)}, u32[]{:S(2)}) collective-permute-start(f32[4,48,128]{2,1,0:T(8,128)S(1)} %bitcast_dynamic-update-slice_fusion.24), channel_id=1, source_target_pairs={{0,6},{2,0},{4,2},{6,4},{1,7},{3,1},{5,3},{7,5},{8,14},{10,8},{12,... | collective-permute-start | bytes 294920 | tf_op jit(solution)/shard_map/ppermute | solution.py:36
  207.6 18.9 %collective-permute-start.31 = (f32[4,48,128]{2,1,0:T(8,128)S(1)}, f32[4,48,128]{2,1,0:T(8,128)S(1)}, u32[]{:S(2)}, u32[]{:S(2)}) collective-permute-start(f32[4,48,128]{2,1,0:T(8,128)S(1)} %bitcast_dynamic-update-slice_fusion.24), channel_id=1, source_target_pairs={{0,4},{2,6},{4,0},{6,2},{1,5},{3,7},{5,1},{7,3},{8,12},{10,14},{12... | collective-permute-start | bytes 294920 | tf_op jit(solution)/shard_map/ppermute | solution.py:36
  207.6 18.9 %collective-permute-start.30 = (f32[4,48,128]{2,1,0:T(8,128)S(1)}, f32[4,48,128]{2,1,0:T(8,128)S(1)}, u32[]{:S(2)}, u32[]{:S(2)}) collective-permute-start(f32[4,48,128]{2,1,0:T(8,128)S(1)} %bitcast_dynamic-update-slice_fusion.24), channel_id=1, source_target_pairs={{0,2},{2,4},{4,6},{6,0},{1,3},{3,5},{5,7},{7,1},{8,10},{10,12},{12... | collective-permute-start | bytes 294920 | tf_op jit(solution)/shard_map/ppermute | solution.py:36
  208.0 17.2 %collective-permute-start.36 = (f32[4,48,128]{2,1,0:T(8,128)S(1)}, f32[4,48,128]{2,1,0:T(8,128)S(1)}, u32[]{:S(2)}, u32[]{:S(2)}) collective-permute-start(f32[4,48,128]{2,1,0:T(8,128)S(1)} %bitcast_dynamic-update-slice_fusion.20), channel_id=1, source_target_pairs={{0,24},{8,0},{16,8},{24,16},{1,25},{9,1},{17,9},{25,17},{2,26},{10... | collective-permute-start | bytes 294920 | tf_op jit(solution)/shard_map/ppermute | solution.py:36
  210.3 19.4 %all-to-all-start.6 = ((f32[32,8,256]{2,1,0:T(8,128)}), f32[32,8,256]{2,1,0:T(8,128)S(1)}, u32[]{:S(2)}, u32[]{:S(2)}) async-start(f32[32,8,256]{2,1,0:T(8,128)} %broadcast_in_dim.220), calls=%async_computation.6 | async-start | bytes 524288 | tf_op jit(solution)/shard_map/all_to_all | solution.py:51
  (26 other events, 157.0 us)

commit v2 on v1

--- a/solution.py
+++ b/solution.py
@@ -80,16 +80,10 @@
 TO_PLANE = [
     (r * 32 + j, (j // 4) * 32 + plane_place((j % 4) * 8 + r)) for r in range(8) for j in range(32)
 ]
-TO_ROWS = [(there, here) for here, there in TO_PLANE]
-
-
-def spread_strip(parts):
-    total = None
-    for r in range(8):
-        moves = [(j, (j // 4) * 32 + plane_place((j % 4) * 8 + r)) for j in range(32)]
-        got = lax.ppermute(parts[r], ALL, moves)
-        total = got if total is None else total + got
-    return total
+
+
+def from_first(parts):
+    return lax.all_to_all(parts, ROW, 0, 0, tiled=True).reshape(parts.shape)[0]
 
 
 def mxu(left, right, left_dim=1, right_dim=0):
@@ -377,11 +371,10 @@
     at = jnp.stack([row_at, col_at]).astype(jnp.int32)
 
     strip = jnp.where((global_cols >= B)[:, None], tile[:B, :].T, zero)
-    panel_part = spread_strip(strip.reshape(8, -1, B))
+    panel_there = from_first(strip.reshape(8, -1, B))
+    panel_part = lax.ppermute(panel_there, ALL, TO_PLANE)
     panel = plane_gather(panel_part)
 
-    panel_part, *panel = lax.optimization_barrier((panel_part, *panel))
-    panel_there = lax.ppermute(panel_part, ALL, TO_ROWS)
     gram, product = products(tile, *panel)
     gram_slice = lax.dynamic_slice_in_dim(gram, place * 8, 8, 0)
     lead_slice = jnp.concatenate(
@@ -402,17 +395,18 @@
 
     edge = tile[B : 2 * B, :].T.reshape(8, -1, B)
     edge, gram = lax.optimization_barrier((edge, gram))
-    edge = lax.all_to_all(edge, ROW, 0, 0, tiled=True)
-    edge = edge.reshape(8, -1, B)[0]
+    edge = from_first(edge)
     upper, inverse = chol(gram)
 
-    u_part = contract(product_part, inverse, 1, 1) - edge
+    part = panel_there.shape[0]
+    both = contract(jnp.concatenate([panel_there, product_part], axis=0), inverse, 1, 1)
+    part_rows = col_at * cols_dev + row_at * part + jnp.arange(part, dtype=jnp.int32)
+    unit_part = (part_rows[:, None] - B == band[None, :]).astype(jnp.float32)
+    u_part = both[part:] - edge
     u_there = lax.ppermute(u_part, ALL, TO_PLANE)
-    both_j = row_gather(jnp.concatenate([panel_there, u_part], axis=1))
+    both_j = row_gather(jnp.concatenate([both[:part] - unit_part, u_part], axis=1))
     t_mat = t_inverse(lead, inverse)
-    unit_j = (global_cols[:, None] - B == band[None, :]).astype(jnp.float32)
-    reflector_j = contract(both_j[:, :B], inverse, 1, 1) - unit_j
-    u_j = both_j[:, B:]
+    reflector_j, u_j = both_j[:, :B], both_j[:, B:]
 
     core_part = contract(reflector_j, u_j, 0, 0).reshape(32, 8, B)
     u_there, core_part = lax.optimization_barrier((u_there, core_part))

time: 242 us -> 249 us (1.029)
  blocking collectives: 23.3 us -> 45.4 us
  starting transfers between devices: 110 us -> 96.8 us
  waiting for transfers between devices: 43.7 us -> 40.7 us
    all_to_all x0 -> x1, blocking collectives: none -> 23.2 us  [from_first(): return lax.all_to_all(parts, ROW, 0, 0, tiled=True).reshape(parts.shape)[0]]
    ppermute x9 -> x1, starting transfers between devices: 28.5 us -> 7.54 us  [per_device(): panel_part = lax.ppermute(panel_there, ALL, TO_PLANE)]
    ppermute x28, starting transfers between devices: 41.7 us -> 48.8 us  [shifted(): lax.ppermute(value, axis, [(k, (k + by) % size) for k in range(size)])]
    ppermute x28, waiting for transfers between devices: 23.1 us -> 20.6 us  [shifted(): lax.ppermute(value, axis, [(k, (k + by) % size) for k in range(size)])]
    dot_general x9 -> x8, matrix products: 8.53 us -> 8.98 us  [contract(): lax.dot_general(left_op, right_op, (((left_dim,), (right_dim,)), ((), ())...]
  transfers between devices with their start and end apart: 43 -> 35, of which waited for: 12 -> 13; matrix products, arithmetic and copies ran while one was open for 5% -> 5% of each run, Pallas kernels for 11% -> 10%
where the time goes in v2:
time: 249 us; the launch traced here: 248 us
  starting transfers between devices  96.8 us (39%)
  blocking collectives  45.4 us (18%)
  waiting for transfers between devices  40.7 us (16%)
  Pallas kernels  39.3 us (16%)
  local copies, waits for them, and re-layouts  12.9 us (5%)
  matrix products  8.98 us (4%)
  other arithmetic  2.66 us (1%)
    ppermute x28, starting transfers between devices, shifted(): lax.ppermute(value, axis, [(k, (k + by) % size) for k in range(size)])  48.8 us
    all_to_all x3, starting transfers between devices, from_everyone(): lax.all_to_all(jnp.broadcast_to(value[None], (size, *value.shape)), axis,...  26.1 us
    pallas_call x2, Pallas kernels, on_squares(): pl.pallas_call(kernel, out_shape=(square,) * outputs, in_specs=[vmem] * l...  25.9 us
    all_to_all x1, blocking collectives, from_first(): return lax.all_to_all(parts, ROW, 0, 0, tiled=True).reshape(parts.shape)[0]  23.2 us
    ppermute x28, waiting for transfers between devices, shifted(): lax.ppermute(value, axis, [(k, (k + by) % size) for k in range(size)])  20.6 us
    all_to_all x1, blocking collectives, per_device(): message = lax.all_to_all(message, ROW, 0, 0, tiled=True)  16.5 us
    all_to_all x3, waiting for transfers between devices, from_everyone(): lax.all_to_all(jnp.broadcast_to(value[None], (size, *value.shape)), axis,...  9.86 us
    dot_general x8, matrix products, contract(): lax.dot_general(left_op, right_op, (((left_dim,), (right_dim,)), ((), ())...  8.98 us
  transfers between devices with their start and end apart: 35, of which 13 were waited for; matrix products, arithmetic and copies ran while one was open for 5% of the time, Pallas kernels for 10%

profile of v2, /device:TPU:1, one launch (start us, length us, event | category | flops | bytes accessed | tf_op | source)
XLA Modules:
  0.0 247.7 jit_solution(2853223651196885306)
XLA Ops:
  1.5 23.2 %all_to_all.40 = f32[8,48,256]{2,1,0:T(8,128)S(1)} all-to-all(f32[8,48,256]{2,1,0:T(8,128)S(1)} %bitcast.142), channel_id=1, replica_groups=mesh['x'=4,'zh'=2,'y'=4,'zl'=4,'c'=2] {'x','zh'}, dimensions={0} | all-to-all | bytes 786432 | tf_op jit(solution)/shard_map/all_to_all | solution.py:86
  24.7 7.5 %collective-permute-start = (f32[48,256]{1,0:T(8,128)S(1)}, f32[48,256]{1,0:T(8,128)S(1)}, u32[]{:S(2)}, u32[]{:S(2)}) collective-permute-start(f32[48,256]{1,0:T(8,128)S(1)} %slice_bitcast_fusion.4), channel_id=1, source_target_pairs={{0,0},{1,16},{2,1},{3,17},{4,32},{5,48},{6,33},{7,49},{8,64},{9,80... | collective-permute-start | bytes 147464 | tf_op jit(solution)/shard_map/ppermute | solution.py:375
  41.3 4.6 %collective-permute-start.2 = (f32[48,128]{1,0:T(8,128)S(1)}, f32[48,128]{1,0:T(8,128)S(1)}, u32[]{:S(2)}, u32[]{:S(2)}) collective-permute-start(f32[48,128]{1,0:T(8,128)S(1)} %get-tuple-element.38), channel_id=1, source_target_pairs={{0,16},{8,24},{16,0},{24,8},{1,17},{9,25},{17,1},{25,9},{2,18},{10... | collective-permute-start | bytes 73736 | tf_op jit(solution)/shard_map/ppermute | solution.py:36
  57.1 4.6 %collective-permute-done.11 = f32[4,48,128]{2,1,0:T(8,128)S(1)} collective-permute-done((f32[4,48,128]{2,1,0:T(8,128)S(1)}, f32[4,48,128]{2,1,0:T(8,128)S(1)}, u32[]{:S(2)}, u32[]{:S(2)}) %collective-permute-start.11) | collective-permute-done | bytes 98336 | tf_op jit(solution)/shard_map/ppermute | solution.py:36
  61.9 5.5 %collective-permute-done.12 = f32[4,48,128]{2,1,0:T(8,128)S(1)} collective-permute-done((f32[4,48,128]{2,1,0:T(8,128)S(1)}, f32[4,48,128]{2,1,0:T(8,128)S(1)}, u32[]{:S(2)}, u32[]{:S(2)}) %collective-permute-start.12) | collective-permute-done | bytes 98336 | tf_op jit(solution)/shard_map/ppermute | solution.py:36
  67.5 7.8 %collective-permute-start.14 = (f32[768,128]{1,0:T(8,128)S(1)}, f32[768,128]{1,0:T(8,128)S(1)}, u32[]{:S(2)}, u32[]{:S(2)}) collective-permute-start(f32[768,128]{1,0:T(8,128)S(1)} %bitcast.147), channel_id=1, source_target_pairs={{0,1},{1,0},{2,3},{3,2},{4,5},{5,4},{6,7},{7,6},{8,9},{9,8},{10,11... | collective-permute-start | bytes 1179656 | tf_op jit(solution)/shard_map/ppermute | solution.py:36
  78.2 4.9 %products.1 = (f32[256,256]{1,0:T(8,128)}, f32[384,256]{1,0:T(8,128)}) custom-call(f32[1536,384]{1,0:T(8,128)} %tile_ref.3, f32[1536,128]{1,0:T(8,128)} %bitcast.151, f32[1536,128]{1,0:T(8,128)} %bitcast.154), custom_call_target="tpu_custom_call" | custom-call | flops 2113929216 | bytes 3932160 | tf_op jit(solution)/shard_map/products/pallas_call | solution.py:259
  85.5 16.5 %all_to_all.42 = f32[8,64,256]{2,1,0:T(8,128)S(1)} all-to-all(f32[8,64,256]{2,1,0:T(8,128)S(1)} %pad_maximum_fusion), channel_id=1, replica_groups=mesh['x'=4,'zh'=2,'y'=4,'zl'=4,'c'=2] {'x','zh'}, dimensions={0} | all-to-all | bytes 1048576 | tf_op jit(solution)/shard_map/all_to_all | solution.py:388
  102.8 10.2 %all-to-all-start.2 = ((f32[16,16,256]{2,1,0:T(8,128)}), f32[16,16,256]{2,1,0:T(8,128)S(1)}, u32[]{:S(2)}, u32[]{:S(2)}) async-start(f32[16,16,256]{2,1,0:T(8,128)} %broadcast_in_dim.197), calls=%async_computation.2 | async-start | bytes 524288 | tf_op jit(solution)/shard_map/all_to_all | solution.py:51
  114.0 9.0 %all-to-all-done.2 = f32[16,16,256]{2,1,0:T(8,128)S(1)} async-done(((f32[16,16,256]{2,1,0:T(8,128)}), f32[16,16,256]{2,1,0:T(8,128)S(1)}, u32[]{:S(2)}, u32[]{:S(2)}) %all-to-all-start.2) | async-done | bytes 262176 | tf_op jit(solution)/shard_map/all_to_all | solution.py:51
  123.1 5.7 %all_to_all.41 = f32[2,16,16,256]{3,2,1,0:T(8,128)S(1)} all-to-all(f32[2,16,16,256]{3,2,1,0:T(8,128)S(1)} %broadcast_in_dim.198), channel_id=1, replica_groups=mesh['x'=4,'zh'=2,'y'=4,'zl'=4,'c'=2] {'c'}, dimensions={0} | all-to-all | bytes 1048576 | tf_op jit(solution)/shard_map/all_to_all | solution.py:51
  129.6 3.5 %all-to-all-start.4 = ((f32[8,48,256]{2,1,0:T(8,128)}), f32[8,48,256]{2,1,0:T(8,128)S(1)}, u32[]{:S(2)}, u32[]{:S(2)}) async-start(f32[8,48,256]{2,1,0:T(8,128)} %bitcast.35), calls=%async_computation.4 | async-start | bytes 786432 | tf_op jit(solution)/shard_map/all_to_all | solution.py:86
  133.1 12.4 %shard_map.17 = (f32[256,256]{1,0:T(8,128)}, f32[256,256]{1,0:T(8,128)}) custom-call(f32[256,256]{1,0:T(8,128)} %get-tuple-element.18.gram_ref), custom_call_target="tpu_custom_call" | custom-call | flops 2000000000 | bytes 1048576 | tf_op jit(solution)/shard_map/pallas_call | solution.py:196
  148.4 8.5 %all-to-all-start.5 = ((f32[8,48,512]{2,1,0:T(8,128)}), f32[8,48,512]{2,1,0:T(8,128)S(1)}, u32[]{:S(2)}, u32[]{:S(2)}) async-start(f32[8,48,512]{2,1,0:T(8,128)} %broadcast_in_dim.199), calls=%async_computation.5 | async-start | bytes 1572864 | tf_op jit(solution)/shard_map/all_to_all | solution.py:51
  159.3 13.5 %shard_map.18 = f32[256,256]{1,0:T(8,128)} custom-call(f32[256,256]{1,0:T(8,128)} %get-tuple-element.29.lead_ref, f32[256,256]{1,0:T(8,128)} %get-tuple-element.19.inverse_ref), custom_call_target="tpu_custom_call" | custom-call | flops 2000000000 | bytes 1048576 | tf_op jit(solution)/shard_map/pallas_call | solution.py:196
  172.7 3.4 %collective-permute-start.15 = (f32[48,256]{1,0:T(8,128)S(1)}, f32[48,256]{1,0:T(8,128)S(1)}, u32[]{:S(2)}, u32[]{:S(2)}) collective-permute-start(f32[48,256]{1,0:T(8,128)S(1)} %get-tuple-element.34), channel_id=1, source_target_pairs={{0,0},{1,16},{2,1},{3,17},{4,32},{5,48},{6,33},{7,49},{8,64},{9,80... | collective-permute-start | bytes 147464 | tf_op jit(solution)/shard_map/ppermute | solution.py:406
  178.5 4.9 %collective-permute-start.20 = (f32[48,128]{1,0:T(8,128)S(1)}, f32[48,128]{1,0:T(8,128)S(1)}, u32[]{:S(2)}, u32[]{:S(2)}) collective-permute-start(f32[48,128]{1,0:T(8,128)S(1)} %get-tuple-element.35), channel_id=1, source_target_pairs={{0,4},{2,6},{4,0},{6,2},{1,5},{3,7},{5,1},{7,3},{8,12},{10,14},{12... | collective-permute-start | bytes 73736 | tf_op jit(solution)/shard_map/ppermute | solution.py:36
  193.7 7.5 %all-to-all-start.6 = ((f32[32,8,256]{2,1,0:T(8,128)}), f32[32,8,256]{2,1,0:T(8,128)S(1)}, u32[]{:S(2)}, u32[]{:S(2)}) async-start(f32[32,8,256]{2,1,0:T(8,128)} %convolution_bitcast_fusion), calls=%async_computation.6 | async-start | bytes 524288 | tf_op jit(solution)/shard_map/all_to_all | solution.py:413
  201.2 2.9 %collective-permute-start.18 = (f32[48,128]{1,0:T(8,128)S(1)}, f32[48,128]{1,0:T(8,128)S(1)}, u32[]{:S(2)}, u32[]{:S(2)}) collective-permute-start(f32[48,128]{1,0:T(8,128)S(1)} %get-tuple-element.36), channel_id=1, source_target_pairs={{0,24},{8,0},{16,8},{24,16},{1,25},{9,1},{17,9},{25,17},{2,26},{10... | collective-permute-start | bytes 73736 | tf_op jit(solution)/shard_map/ppermute | solution.py:36
  205.1 7.4 %all-to-all-done.6 = f32[32,8,256]{2,1,0:T(8,128)S(1)} async-done(((f32[32,8,256]{2,1,0:T(8,128)}), f32[32,8,256]{2,1,0:T(8,128)S(1)}, u32[]{:S(2)}, u32[]{:S(2)}) %all-to-all-start.6) | async-done | bytes 262176 | tf_op jit(solution)/shard_map/all_to_all | solution.py:413
  216.4 7.3 %all-to-all-start.7 = ((f32[32,8,256]{2,1,0:T(8,128)}), f32[32,8,256]{2,1,0:T(8,128)S(1)}, u32[]{:S(2)}, u32[]{:S(2)}) async-start(f32[32,8,256]{2,1,0:T(8,128)} %broadcast_in_dim.220), calls=%async_computation.7 | async-start | bytes 524288 | tf_op jit(solution)/shard_map/all_to_all | solution.py:51
  223.8 3.0 %collective-permute-start.27 = (f32[4,48,128]{2,1,0:T(8,128)S(1)}, f32[4,48,128]{2,1,0:T(8,128)S(1)}, u32[]{:S(2)}, u32[]{:S(2)}) collective-permute-start(f32[4,48,128]{2,1,0:T(8,128)S(1)} %bitcast_dynamic-update-slice_fusion.20), channel_id=1, source_target_pairs={{0,16},{8,24},{16,0},{24,8},{1,17},{9,25},{17,1},{25,9},{2,18},{10... | collective-permute-start | bytes 294920 | tf_op jit(solution)/shard_map/ppermute | solution.py:36
  226.8 4.5 %collective-permute-done.27 = f32[4,48,128]{2,1,0:T(8,128)S(1)} collective-permute-done((f32[4,48,128]{2,1,0:T(8,128)S(1)}, f32[4,48,128]{2,1,0:T(8,128)S(1)}, u32[]{:S(2)}, u32[]{:S(2)}) %collective-permute-start.27) | collective-permute-done | bytes 98336 | tf_op jit(solution)/shard_map/ppermute | solution.py:36
  239.1 8.5 %update.1 = f32[1536,384]{1,0:T(8,128)} custom-call(s32[2]{0:T(128)} %pad_add_fusion.at_ref, f32[1536,384]{1,0:T(8,128)} %tile_ref.3, f32[1536,128]{1,0:T(8,128)} %bitcast.153, f32[1536,128]{1,0:T(8,128)} %bitcast.156, f32[1536,128]{1,0:T(8,128)} %bitcast.60.ul_ref, f32[1536,128]{1,0:T(8,128)} %bitcast.157, f32[256,384]{1,0:T(8,128)} %fusion.19.f_ref, ...), custom_call_target="tpu_custom_call" | custom-call | flops 2717908992 | bytes 7864320 | tf_op jit(solution)/shard_map/update/pallas_call | solution.py:337
  (160 shorter events, 59.8 us)
Async XLA Ops:
  24.7 10.2 %collective-permute-start = (f32[48,256]{1,0:T(8,128)S(1)}, f32[48,256]{1,0:T(8,128)S(1)}, u32[]{:S(2)}, u32[]{:S(2)}) collective-permute-start(f32[48,256]{1,0:T(8,128)S(1)} %slice_bitcast_fusion.4), channel_id=1, source_target_pairs={{0,0},{1,16},{2,1},{3,17},{4,32},{5,48},{6,33},{7,49},{8,64},{9,80... | collective-permute-start | bytes 147464 | tf_op jit(solution)/shard_map/ppermute | solution.py:375
  34.9 19.9 %collective-permute-start.9 = (f32[48,128]{1,0:T(8,128)S(1)}, f32[48,128]{1,0:T(8,128)S(1)}, u32[]{:S(2)}, u32[]{:S(2)}) collective-permute-start(f32[48,128]{1,0:T(8,128)S(1)} %get-tuple-element.37), channel_id=1, source_target_pairs={{0,4},{2,6},{4,0},{6,2},{1,5},{3,7},{5,1},{7,3},{8,12},{10,14},{12... | collective-permute-start | bytes 73736 | tf_op jit(solution)/shard_map/ppermute | solution.py:36
  36.6 17.9 %collective-permute-start.8 = (f32[48,128]{1,0:T(8,128)S(1)}, f32[48,128]{1,0:T(8,128)S(1)}, u32[]{:S(2)}, u32[]{:S(2)}) collective-permute-start(f32[48,128]{1,0:T(8,128)S(1)} %get-tuple-element.37), channel_id=1, source_target_pairs={{0,2},{2,4},{4,6},{6,0},{1,3},{3,5},{5,7},{7,1},{8,10},{10,12},{12... | collective-permute-start | bytes 73736 | tf_op jit(solution)/shard_map/ppermute | solution.py:36
  39.3 15.5 %collective-permute-start.10 = (f32[48,128]{1,0:T(8,128)S(1)}, f32[48,128]{1,0:T(8,128)S(1)}, u32[]{:S(2)}, u32[]{:S(2)}) collective-permute-start(f32[48,128]{1,0:T(8,128)S(1)} %get-tuple-element.37), channel_id=1, source_target_pairs={{0,6},{2,0},{4,2},{6,4},{1,7},{3,1},{5,3},{7,5},{8,14},{10,8},{12,... | collective-permute-start | bytes 73736 | tf_op jit(solution)/shard_map/ppermute | solution.py:36
  41.3 9.9 %collective-permute-start.2 = (f32[48,128]{1,0:T(8,128)S(1)}, f32[48,128]{1,0:T(8,128)S(1)}, u32[]{:S(2)}, u32[]{:S(2)}) collective-permute-start(f32[48,128]{1,0:T(8,128)S(1)} %get-tuple-element.38), channel_id=1, source_target_pairs={{0,16},{8,24},{16,0},{24,8},{1,17},{9,25},{17,1},{25,9},{2,18},{10... | collective-permute-start | bytes 73736 | tf_op jit(solution)/shard_map/ppermute | solution.py:36
  53.1 22.3 %collective-permute-start.6 = (f32[4,48,128]{2,1,0:T(8,128)S(1)}, f32[4,48,128]{2,1,0:T(8,128)S(1)}, u32[]{:S(2)}, u32[]{:S(2)}) collective-permute-start(f32[4,48,128]{2,1,0:T(8,128)S(1)} %bitcast_dynamic-update-slice_fusion.32), channel_id=1, source_target_pairs={{0,6},{2,0},{4,2},{6,4},{1,7},{3,1},{5,3},{7,5},{8,14},{10,8},{12,... | collective-permute-start | bytes 294920 | tf_op jit(solution)/shard_map/ppermute | solution.py:36
  54.5 20.9 %collective-permute-start.5 = (f32[4,48,128]{2,1,0:T(8,128)S(1)}, f32[4,48,128]{2,1,0:T(8,128)S(1)}, u32[]{:S(2)}, u32[]{:S(2)}) collective-permute-start(f32[4,48,128]{2,1,0:T(8,128)S(1)} %bitcast_dynamic-update-slice_fusion.32), channel_id=1, source_target_pairs={{0,4},{2,6},{4,0},{6,2},{1,5},{3,7},{5,1},{7,3},{8,12},{10,14},{12... | collective-permute-start | bytes 294920 | tf_op jit(solution)/shard_map/ppermute | solution.py:36
  54.5 20.9 %collective-permute-start.4 = (f32[4,48,128]{2,1,0:T(8,128)S(1)}, f32[4,48,128]{2,1,0:T(8,128)S(1)}, u32[]{:S(2)}, u32[]{:S(2)}) collective-permute-start(f32[4,48,128]{2,1,0:T(8,128)S(1)} %bitcast_dynamic-update-slice_fusion.32), channel_id=1, source_target_pairs={{0,2},{2,4},{4,6},{6,0},{1,3},{3,5},{5,7},{7,1},{8,10},{10,12},{12... | collective-permute-start | bytes 294920 | tf_op jit(solution)/shard_map/ppermute | solution.py:36
  54.8 12.7 %collective-permute-start.13 = (f32[4,48,128]{2,1,0:T(8,128)S(1)}, f32[4,48,128]{2,1,0:T(8,128)S(1)}, u32[]{:S(2)}, u32[]{:S(2)}) collective-permute-start(f32[4,48,128]{2,1,0:T(8,128)S(1)} %bitcast_dynamic-update-slice_fusion.28), channel_id=1, source_target_pairs={{0,24},{8,0},{16,8},{24,16},{1,25},{9,1},{17,9},{25,17},{2,26},{10... | collective-permute-start | bytes 294920 | tf_op jit(solution)/shard_map/ppermute | solution.py:36
  67.5 9.2 %collective-permute-start.14 = (f32[768,128]{1,0:T(8,128)S(1)}, f32[768,128]{1,0:T(8,128)S(1)}, u32[]{:S(2)}, u32[]{:S(2)}) collective-permute-start(f32[768,128]{1,0:T(8,128)S(1)} %bitcast.147), channel_id=1, source_target_pairs={{0,1},{1,0},{2,3},{3,2},{4,5},{5,4},{6,7},{7,6},{8,9},{9,8},{10,11... | collective-permute-start | bytes 1179656 | tf_op jit(solution)/shard_map/ppermute | solution.py:36
  102.8 20.2 %all-to-all-start.2 = ((f32[16,16,256]{2,1,0:T(8,128)}), f32[16,16,256]{2,1,0:T(8,128)S(1)}, u32[]{:S(2)}, u32[]{:S(2)}) async-start(f32[16,16,256]{2,1,0:T(8,128)} %broadcast_in_dim.197), calls=%async_computation.2 | async-start | bytes 524288 | tf_op jit(solution)/shard_map/all_to_all | solution.py:51
  129.6 17.7 %all-to-all-start.4 = ((f32[8,48,256]{2,1,0:T(8,128)}), f32[8,48,256]{2,1,0:T(8,128)S(1)}, u32[]{:S(2)}, u32[]{:S(2)}) async-start(f32[8,48,256]{2,1,0:T(8,128)} %bitcast.35), calls=%async_computation.4 | async-start | bytes 786432 | tf_op jit(solution)/shard_map/all_to_all | solution.py:86
  148.4 28.6 %all-to-all-start.5 = ((f32[8,48,512]{2,1,0:T(8,128)}), f32[8,48,512]{2,1,0:T(8,128)S(1)}, u32[]{:S(2)}, u32[]{:S(2)}) async-start(f32[8,48,512]{2,1,0:T(8,128)} %broadcast_in_dim.199), calls=%async_computation.5 | async-start | bytes 1572864 | tf_op jit(solution)/shard_map/all_to_all | solution.py:51
  178.5 25.6 %collective-permute-start.20 = (f32[48,128]{1,0:T(8,128)S(1)}, f32[48,128]{1,0:T(8,128)S(1)}, u32[]{:S(2)}, u32[]{:S(2)}) collective-permute-start(f32[48,128]{1,0:T(8,128)S(1)} %get-tuple-element.35), channel_id=1, source_target_pairs={{0,4},{2,6},{4,0},{6,2},{1,5},{3,7},{5,1},{7,3},{8,12},{10,14},{12... | collective-permute-start | bytes 73736 | tf_op jit(solution)/shard_map/ppermute | solution.py:36
  183.5 17.8 %collective-permute-start.19 = (f32[48,128]{1,0:T(8,128)S(1)}, f32[48,128]{1,0:T(8,128)S(1)}, u32[]{:S(2)}, u32[]{:S(2)}) collective-permute-start(f32[48,128]{1,0:T(8,128)S(1)} %get-tuple-element.35), channel_id=1, source_target_pairs={{0,2},{2,4},{4,6},{6,0},{1,3},{3,5},{5,7},{7,1},{8,10},{10,12},{12... | collective-permute-start | bytes 73736 | tf_op jit(solution)/shard_map/ppermute | solution.py:36
  184.1 20.0 %collective-permute-start.21 = (f32[48,128]{1,0:T(8,128)S(1)}, f32[48,128]{1,0:T(8,128)S(1)}, u32[]{:S(2)}, u32[]{:S(2)}) collective-permute-start(f32[48,128]{1,0:T(8,128)S(1)} %get-tuple-element.35), channel_id=1, source_target_pairs={{0,6},{2,0},{4,2},{6,4},{1,7},{3,1},{5,3},{7,5},{8,14},{10,8},{12,... | collective-permute-start | bytes 73736 | tf_op jit(solution)/shard_map/ppermute | solution.py:36
  186.7 17.5 %collective-permute-start.17 = (f32[48,128]{1,0:T(8,128)S(1)}, f32[48,128]{1,0:T(8,128)S(1)}, u32[]{:S(2)}, u32[]{:S(2)}) collective-permute-start(f32[48,128]{1,0:T(8,128)S(1)} %get-tuple-element.36), channel_id=1, source_target_pairs={{0,16},{8,24},{16,0},{24,8},{1,17},{9,25},{17,1},{25,9},{2,18},{10... | collective-permute-start | bytes 73736 | tf_op jit(solution)/shard_map/ppermute | solution.py:36
  189.4 14.8 %collective-permute-start.16 = (f32[48,128]{1,0:T(8,128)S(1)}, f32[48,128]{1,0:T(8,128)S(1)}, u32[]{:S(2)}, u32[]{:S(2)}) collective-permute-start(f32[48,128]{1,0:T(8,128)S(1)} %get-tuple-element.36), channel_id=1, source_target_pairs={{0,8},{8,16},{16,24},{24,0},{1,9},{9,17},{17,25},{25,1},{2,10},{10... | collective-permute-start | bytes 73736 | tf_op jit(solution)/shard_map/ppermute | solution.py:36
  193.7 18.7 %all-to-all-start.6 = ((f32[32,8,256]{2,1,0:T(8,128)}), f32[32,8,256]{2,1,0:T(8,128)S(1)}, u32[]{:S(2)}, u32[]{:S(2)}) async-start(f32[32,8,256]{2,1,0:T(8,128)} %convolution_bitcast_fusion), calls=%async_computation.6 | async-start | bytes 524288 | tf_op jit(solution)/shard_map/all_to_all | solution.py:413
  212.5 20.2 %collective-permute-start.24 = (f32[4,48,128]{2,1,0:T(8,128)S(1)}, f32[4,48,128]{2,1,0:T(8,128)S(1)}, u32[]{:S(2)}, u32[]{:S(2)}) collective-permute-start(f32[4,48,128]{2,1,0:T(8,128)S(1)} %bitcast_dynamic-update-slice_fusion.24), channel_id=1, source_target_pairs={{0,6},{2,0},{4,2},{6,4},{1,7},{3,1},{5,3},{7,5},{8,14},{10,8},{12,... | collective-permute-start | bytes 294920 | tf_op jit(solution)/shard_map/ppermute | solution.py:36
  213.7 18.9 %collective-permute-start.23 = (f32[4,48,128]{2,1,0:T(8,128)S(1)}, f32[4,48,128]{2,1,0:T(8,128)S(1)}, u32[]{:S(2)}, u32[]{:S(2)}) collective-permute-start(f32[4,48,128]{2,1,0:T(8,128)S(1)} %bitcast_dynamic-update-slice_fusion.24), channel_id=1, source_target_pairs={{0,4},{2,6},{4,0},{6,2},{1,5},{3,7},{5,1},{7,3},{8,12},{10,14},{12... | collective-permute-start | bytes 294920 | tf_op jit(solution)/shard_map/ppermute | solution.py:36
  213.7 18.9 %collective-permute-start.22 = (f32[4,48,128]{2,1,0:T(8,128)S(1)}, f32[4,48,128]{2,1,0:T(8,128)S(1)}, u32[]{:S(2)}, u32[]{:S(2)}) collective-permute-start(f32[4,48,128]{2,1,0:T(8,128)S(1)} %bitcast_dynamic-update-slice_fusion.24), channel_id=1, source_target_pairs={{0,2},{2,4},{4,6},{6,0},{1,3},{3,5},{5,7},{7,1},{8,10},{10,12},{12... | collective-permute-start | bytes 294920 | tf_op jit(solution)/shard_map/ppermute | solution.py:36
  214.1 17.2 %collective-permute-start.28 = (f32[4,48,128]{2,1,0:T(8,128)S(1)}, f32[4,48,128]{2,1,0:T(8,128)S(1)}, u32[]{:S(2)}, u32[]{:S(2)}) collective-permute-start(f32[4,48,128]{2,1,0:T(8,128)S(1)} %bitcast_dynamic-update-slice_fusion.20), channel_id=1, source_target_pairs={{0,24},{8,0},{16,8},{24,16},{1,25},{9,1},{17,9},{25,17},{2,26},{10... | collective-permute-start | bytes 294920 | tf_op jit(solution)/shard_map/ppermute | solution.py:36
  216.4 19.9 %all-to-all-start.7 = ((f32[32,8,256]{2,1,0:T(8,128)}), f32[32,8,256]{2,1,0:T(8,128)S(1)}, u32[]{:S(2)}, u32[]{:S(2)}) async-start(f32[32,8,256]{2,1,0:T(8,128)} %broadcast_in_dim.220), calls=%async_computation.7 | async-start | bytes 524288 | tf_op jit(solution)/shard_map/all_to_all | solution.py:51
  (20 other events, 133.6 us)

commit v3 on v1

--- a/solution.py
+++ b/solution.py
@@ -380,8 +380,6 @@
     panel_part = spread_strip(strip.reshape(8, -1, B))
     panel = plane_gather(panel_part)
 
-    panel_part, *panel = lax.optimization_barrier((panel_part, *panel))
-    panel_there = lax.ppermute(panel_part, ALL, TO_ROWS)
     gram, product = products(tile, *panel)
     gram_slice = lax.dynamic_slice_in_dim(gram, place * 8, 8, 0)
     lead_slice = jnp.concatenate(
@@ -401,18 +399,21 @@
     lead = message[:, 1].reshape(B, B)
 
     edge = tile[B : 2 * B, :].T.reshape(8, -1, B)
-    edge, gram = lax.optimization_barrier((edge, gram))
+    edge, panel_part, gram = lax.optimization_barrier((edge, panel_part, gram))
     edge = lax.all_to_all(edge, ROW, 0, 0, tiled=True)
     edge = edge.reshape(8, -1, B)[0]
+    panel_there = lax.ppermute(panel_part, ALL, TO_ROWS)
     upper, inverse = chol(gram)
 
-    u_part = contract(product_part, inverse, 1, 1) - edge
+    part = panel_there.shape[0]
+    both = contract(jnp.concatenate([panel_there, product_part], axis=0), inverse, 1, 1)
+    part_rows = col_at * cols_dev + row_at * part + jnp.arange(part, dtype=jnp.int32)
+    unit_part = (part_rows[:, None] - B == band[None, :]).astype(jnp.float32)
+    u_part = both[part:] - edge
     u_there = lax.ppermute(u_part, ALL, TO_PLANE)
-    both_j = row_gather(jnp.concatenate([panel_there, u_part], axis=1))
+    both_j = row_gather(jnp.concatenate([both[:part] - unit_part, u_part], axis=1))
     t_mat = t_inverse(lead, inverse)
-    unit_j = (global_cols[:, None] - B == band[None, :]).astype(jnp.float32)
-    reflector_j = contract(both_j[:, :B], inverse, 1, 1) - unit_j
-    u_j = both_j[:, B:]
+    reflector_j, u_j = both_j[:, :B], both_j[:, B:]
 
     core_part = contract(reflector_j, u_j, 0, 0).reshape(32, 8, B)
     u_there, core_part = lax.optimization_barrier((u_there, core_part))

time: 242 us -> 244 us (level)
    dot_general x9 -> x8, matrix products: 8.53 us -> 8.98 us  [contract(): lax.dot_general(left_op, right_op, (((left_dim,), (right_dim,)), ((), ())...]
  transfers between devices with their start and end apart: 43 -> 43, of which waited for: 12 -> 12; matrix products, arithmetic and copies ran while one was open for 5% -> 6% of each run, Pallas kernels for 11% -> 11%
where the time goes in v3:
time: 244 us; the launch traced here: 243 us
  starting transfers between devices  110 us (45%)
  waiting for transfers between devices  44.3 us (18%)
  Pallas kernels  39.3 us (16%)
  blocking collectives  23.3 us (10%)
  local copies, waits for them, and re-layouts  13.1 us (5%)
  matrix products  8.98 us (4%)
  other arithmetic  2.68 us (1%)
    ppermute x28, starting transfers between devices, shifted(): lax.ppermute(value, axis, [(k, (k + by) % size) for k in range(size)])  41.7 us
    ppermute x8, starting transfers between devices, spread_strip(): got = lax.ppermute(parts[r], ALL, moves)  26.4 us
    all_to_all x3, starting transfers between devices, from_everyone(): lax.all_to_all(jnp.broadcast_to(value[None], (size, *value.shape)), axis,...  25.9 us
    pallas_call x2, Pallas kernels, on_squares(): pl.pallas_call(kernel, out_shape=(square,) * outputs, in_specs=[vmem] * l...  25.9 us
    ppermute x28, waiting for transfers between devices, shifted(): lax.ppermute(value, axis, [(k, (k + by) % size) for k in range(size)])  23.1 us
    all_to_all x1, blocking collectives, per_device(): message = lax.all_to_all(message, ROW, 0, 0, tiled=True)  17.6 us
    all_to_all x3, waiting for transfers between devices, from_everyone(): lax.all_to_all(jnp.broadcast_to(value[None], (size, *value.shape)), axis,...  9.01 us
    dot_general x8, matrix products, contract(): lax.dot_general(left_op, right_op, (((left_dim,), (right_dim,)), ((), ())...  8.98 us
  transfers between devices with their start and end apart: 43, of which 12 were waited for; matrix products, arithmetic and copies ran while one was open for 6% of the time, Pallas kernels for 11%

profile of v3, /device:TPU:1, one launch (start us, length us, event | category | flops | bytes accessed | tf_op | source)
XLA Modules:
  0.0 243.2 jit_solution(13059556646057819119)
XLA Ops:
  1.5 7.6 %collective-permute-start.1 = (f32[48,256]{1,0:T(8,128)S(1)}, f32[48,256]{1,0:T(8,128)S(1)}, u32[]{:S(2)}, u32[]{:S(2)}) collective-permute-start(f32[48,256]{1,0:T(8,128)S(1)} %get-tuple-element.33), channel_id=1, source_target_pairs={{0,2},{1,18},{2,3},{3,19},{4,34},{5,50},{6,35},{7,51},{8,66},{9,82... | collective-permute-start | bytes 147464 | tf_op jit(solution)/shard_map/ppermute | solution.py:90
  9.1 9.3 %collective-permute-start.7 = (f32[48,256]{1,0:T(8,128)S(1)}, f32[48,256]{1,0:T(8,128)S(1)}, u32[]{:S(2)}, u32[]{:S(2)}) collective-permute-start(f32[48,256]{1,0:T(8,128)S(1)} %get-tuple-element.34), channel_id=1, source_target_pairs={{0,14},{1,30},{2,15},{3,31},{4,46},{5,62},{6,47},{7,63},{8,78},{9,... | collective-permute-start | bytes 147464 | tf_op jit(solution)/shard_map/ppermute | solution.py:90
  28.2 3.2 %collective-permute-done = f32[48,256]{1,0:T(8,128)S(1)} collective-permute-done((f32[48,256]{1,0:T(8,128)S(1)}, f32[48,256]{1,0:T(8,128)S(1)}, u32[]{:S(2)}, u32[]{:S(2)}) %collective-permute-start) | collective-permute-done | bytes 49184 | tf_op jit(solution)/shard_map/ppermute | solution.py:90
  31.7 3.3 %collective-permute-start.17 = (f32[48,128]{1,0:T(8,128)S(1)}, f32[48,128]{1,0:T(8,128)S(1)}, u32[]{:S(2)}, u32[]{:S(2)}) collective-permute-start(f32[48,128]{1,0:T(8,128)S(1)} %get-tuple-element.47), channel_id=1, source_target_pairs={{0,6},{2,0},{4,2},{6,4},{1,7},{3,1},{5,3},{7,5},{8,14},{10,8},{12,... | collective-permute-start | bytes 73736 | tf_op jit(solution)/shard_map/ppermute | solution.py:36
  36.3 3.8 %collective-permute-done.8 = f32[48,128]{1,0:T(8,128)S(1)} collective-permute-done((f32[48,128]{1,0:T(8,128)S(1)}, f32[48,128]{1,0:T(8,128)S(1)}, u32[]{:S(2)}, u32[]{:S(2)}) %collective-permute-start.8) | collective-permute-done | bytes 24608 | tf_op jit(solution)/shard_map/ppermute | solution.py:36
  46.5 4.7 %collective-permute-done.18 = f32[4,48,128]{2,1,0:T(8,128)S(1)} collective-permute-done((f32[4,48,128]{2,1,0:T(8,128)S(1)}, f32[4,48,128]{2,1,0:T(8,128)S(1)}, u32[]{:S(2)}, u32[]{:S(2)}) %collective-permute-start.18) | collective-permute-done | bytes 98336 | tf_op jit(solution)/shard_map/ppermute | solution.py:36
  51.2 5.1 %collective-permute-done.19 = f32[4,48,128]{2,1,0:T(8,128)S(1)} collective-permute-done((f32[4,48,128]{2,1,0:T(8,128)S(1)}, f32[4,48,128]{2,1,0:T(8,128)S(1)}, u32[]{:S(2)}, u32[]{:S(2)}) %collective-permute-start.19) | collective-permute-done | bytes 98336 | tf_op jit(solution)/shard_map/ppermute | solution.py:36
  56.3 7.8 %collective-permute-start.21 = (f32[768,128]{1,0:T(8,128)S(1)}, f32[768,128]{1,0:T(8,128)S(1)}, u32[]{:S(2)}, u32[]{:S(2)}) collective-permute-start(f32[768,128]{1,0:T(8,128)S(1)} %bitcast.143), channel_id=1, source_target_pairs={{0,1},{1,0},{2,3},{3,2},{4,5},{5,4},{6,7},{7,6},{8,9},{9,8},{10,11... | collective-permute-start | bytes 1179656 | tf_op jit(solution)/shard_map/ppermute | solution.py:36
  67.1 4.9 %products.1 = (f32[256,256]{1,0:T(8,128)}, f32[384,256]{1,0:T(8,128)}) custom-call(f32[1536,384]{1,0:T(8,128)} %tile_ref.3, f32[1536,128]{1,0:T(8,128)} %bitcast.147, f32[1536,128]{1,0:T(8,128)} %bitcast.150), custom_call_target="tpu_custom_call" | custom-call | flops 2113929216 | bytes 3932160 | tf_op jit(solution)/shard_map/products/pallas_call | solution.py:265
  74.5 17.6 %all_to_all.36 = f32[8,64,256]{2,1,0:T(8,128)S(1)} all-to-all(f32[8,64,256]{2,1,0:T(8,128)S(1)} %pad_maximum_fusion), channel_id=1, replica_groups=mesh['x'=4,'zh'=2,'y'=4,'zl'=4,'c'=2] {'x','zh'}, dimensions={0} | all-to-all | bytes 1048576 | tf_op jit(solution)/shard_map/all_to_all | solution.py:393
  92.9 9.8 %all-to-all-start.1 = ((f32[16,16,256]{2,1,0:T(8,128)}), f32[16,16,256]{2,1,0:T(8,128)S(1)}, u32[]{:S(2)}, u32[]{:S(2)}) async-start(f32[16,16,256]{2,1,0:T(8,128)} %broadcast_in_dim.197), calls=%async_computation.1 | async-start | bytes 524288 | tf_op jit(solution)/shard_map/all_to_all | solution.py:51
  103.6 9.0 %all-to-all-done.1 = f32[16,16,256]{2,1,0:T(8,128)S(1)} async-done(((f32[16,16,256]{2,1,0:T(8,128)}), f32[16,16,256]{2,1,0:T(8,128)S(1)}, u32[]{:S(2)}, u32[]{:S(2)}) %all-to-all-start.1) | async-done | bytes 262176 | tf_op jit(solution)/shard_map/all_to_all | solution.py:51
  112.7 5.7 %all_to_all.35 = f32[2,16,16,256]{3,2,1,0:T(8,128)S(1)} all-to-all(f32[2,16,16,256]{3,2,1,0:T(8,128)S(1)} %broadcast_in_dim.198), channel_id=1, replica_groups=mesh['x'=4,'zh'=2,'y'=4,'zl'=4,'c'=2] {'c'}, dimensions={0} | all-to-all | bytes 1048576 | tf_op jit(solution)/shard_map/all_to_all | solution.py:51
  119.3 3.5 %all-to-all-start.3 = ((f32[8,48,256]{2,1,0:T(8,128)}), f32[8,48,256]{2,1,0:T(8,128)S(1)}, u32[]{:S(2)}, u32[]{:S(2)}) async-start(f32[8,48,256]{2,1,0:T(8,128)} %bitcast.32), calls=%async_computation.3 | async-start | bytes 786432 | tf_op jit(solution)/shard_map/all_to_all | solution.py:403
  125.0 12.4 %shard_map.17 = (f32[256,256]{1,0:T(8,128)}, f32[256,256]{1,0:T(8,128)}) custom-call(f32[256,256]{1,0:T(8,128)} %get-tuple-element.20.gram_ref), custom_call_target="tpu_custom_call" | custom-call | flops 2000000000 | bytes 1048576 | tf_op jit(solution)/shard_map/pallas_call | solution.py:202
  139.9 8.8 %all-to-all-start.4 = ((f32[8,48,512]{2,1,0:T(8,128)}), f32[8,48,512]{2,1,0:T(8,128)S(1)}, u32[]{:S(2)}, u32[]{:S(2)}) async-start(f32[8,48,512]{2,1,0:T(8,128)} %broadcast_in_dim.199), calls=%async_computation.4 | async-start | bytes 1572864 | tf_op jit(solution)/shard_map/all_to_all | solution.py:51
  150.9 13.5 %shard_map.18 = f32[256,256]{1,0:T(8,128)} custom-call(f32[256,256]{1,0:T(8,128)} %get-tuple-element.31.lead_ref, f32[256,256]{1,0:T(8,128)} %get-tuple-element.21.inverse_ref), custom_call_target="tpu_custom_call" | custom-call | flops 2000000000 | bytes 1048576 | tf_op jit(solution)/shard_map/pallas_call | solution.py:202
  164.4 3.4 %collective-permute-start.23 = (f32[48,256]{1,0:T(8,128)S(1)}, f32[48,256]{1,0:T(8,128)S(1)}, u32[]{:S(2)}, u32[]{:S(2)}) collective-permute-start(f32[48,256]{1,0:T(8,128)S(1)} %get-tuple-element.44), channel_id=1, source_target_pairs={{0,0},{1,16},{2,1},{3,17},{4,32},{5,48},{6,33},{7,49},{8,64},{9,80... | collective-permute-start | bytes 147464 | tf_op jit(solution)/shard_map/ppermute | solution.py:413
  170.7 6.5 %collective-permute-start.28 = (f32[48,128]{1,0:T(8,128)S(1)}, f32[48,128]{1,0:T(8,128)S(1)}, u32[]{:S(2)}, u32[]{:S(2)}) collective-permute-start(f32[48,128]{1,0:T(8,128)S(1)} %get-tuple-element.45), channel_id=1, source_target_pairs={{0,4},{2,6},{4,0},{6,2},{1,5},{3,7},{5,1},{7,3},{8,12},{10,14},{12... | collective-permute-start | bytes 73736 | tf_op jit(solution)/shard_map/ppermute | solution.py:36
  189.0 7.4 %all-to-all-start.5 = ((f32[32,8,256]{2,1,0:T(8,128)}), f32[32,8,256]{2,1,0:T(8,128)S(1)}, u32[]{:S(2)}, u32[]{:S(2)}) async-start(f32[32,8,256]{2,1,0:T(8,128)} %convolution_bitcast_fusion), calls=%async_computation.5 | async-start | bytes 524288 | tf_op jit(solution)/shard_map/all_to_all | solution.py:420
  200.0 7.6 %all-to-all-done.5 = f32[32,8,256]{2,1,0:T(8,128)S(1)} async-done(((f32[32,8,256]{2,1,0:T(8,128)}), f32[32,8,256]{2,1,0:T(8,128)S(1)}, u32[]{:S(2)}, u32[]{:S(2)}) %all-to-all-start.5) | async-done | bytes 262176 | tf_op jit(solution)/shard_map/all_to_all | solution.py:420
  211.6 7.4 %all-to-all-start.6 = ((f32[32,8,256]{2,1,0:T(8,128)}), f32[32,8,256]{2,1,0:T(8,128)S(1)}, u32[]{:S(2)}, u32[]{:S(2)}) async-start(f32[32,8,256]{2,1,0:T(8,128)} %broadcast_in_dim.220), calls=%async_computation.6 | async-start | bytes 524288 | tf_op jit(solution)/shard_map/all_to_all | solution.py:51
  221.9 4.5 %collective-permute-done.35 = f32[4,48,128]{2,1,0:T(8,128)S(1)} collective-permute-done((f32[4,48,128]{2,1,0:T(8,128)S(1)}, f32[4,48,128]{2,1,0:T(8,128)S(1)}, u32[]{:S(2)}, u32[]{:S(2)}) %collective-permute-start.35) | collective-permute-done | bytes 98336 | tf_op jit(solution)/shard_map/ppermute | solution.py:36
  234.6 8.5 %update.1 = f32[1536,384]{1,0:T(8,128)} custom-call(s32[2]{0:T(128)} %pad_add_fusion.at_ref, f32[1536,384]{1,0:T(8,128)} %tile_ref.3, f32[1536,128]{1,0:T(8,128)} %bitcast.149, f32[1536,128]{1,0:T(8,128)} %bitcast.152, f32[1536,128]{1,0:T(8,128)} %bitcast.58.ul_ref, f32[1536,128]{1,0:T(8,128)} %bitcast.153, f32[256,384]{1,0:T(8,128)} %fusion.20.f_ref, ...), custom_call_target="tpu_custom_call" | custom-call | flops 2717908992 | bytes 7864320 | tf_op jit(solution)/shard_map/update/pallas_call | solution.py:343
  (176 shorter events, 67.0 us)
Async XLA Ops:
  1.5 21.7 %collective-permute-start.1 = (f32[48,256]{1,0:T(8,128)S(1)}, f32[48,256]{1,0:T(8,128)S(1)}, u32[]{:S(2)}, u32[]{:S(2)}) collective-permute-start(f32[48,256]{1,0:T(8,128)S(1)} %get-tuple-element.33), channel_id=1, source_target_pairs={{0,2},{1,18},{2,3},{3,19},{4,34},{5,50},{6,35},{7,51},{8,66},{9,82... | collective-permute-start | bytes 147464 | tf_op jit(solution)/shard_map/ppermute | solution.py:90
  9.1 15.5 %collective-permute-start.7 = (f32[48,256]{1,0:T(8,128)S(1)}, f32[48,256]{1,0:T(8,128)S(1)}, u32[]{:S(2)}, u32[]{:S(2)}) collective-permute-start(f32[48,256]{1,0:T(8,128)S(1)} %get-tuple-element.34), channel_id=1, source_target_pairs={{0,14},{1,30},{2,15},{3,31},{4,46},{5,62},{6,47},{7,63},{8,78},{9,... | collective-permute-start | bytes 147464 | tf_op jit(solution)/shard_map/ppermute | solution.py:90
  31.5 13.1 %collective-permute-start.16 = (f32[48,128]{1,0:T(8,128)S(1)}, f32[48,128]{1,0:T(8,128)S(1)}, u32[]{:S(2)}, u32[]{:S(2)}) collective-permute-start(f32[48,128]{1,0:T(8,128)S(1)} %get-tuple-element.47), channel_id=1, source_target_pairs={{0,4},{2,6},{4,0},{6,2},{1,5},{3,7},{5,1},{7,3},{8,12},{10,14},{12... | collective-permute-start | bytes 73736 | tf_op jit(solution)/shard_map/ppermute | solution.py:36
  31.6 11.5 %collective-permute-start.15 = (f32[48,128]{1,0:T(8,128)S(1)}, f32[48,128]{1,0:T(8,128)S(1)}, u32[]{:S(2)}, u32[]{:S(2)}) collective-permute-start(f32[48,128]{1,0:T(8,128)S(1)} %get-tuple-element.47), channel_id=1, source_target_pairs={{0,2},{2,4},{4,6},{6,0},{1,3},{3,5},{5,7},{7,1},{8,10},{10,12},{12... | collective-permute-start | bytes 73736 | tf_op jit(solution)/shard_map/ppermute | solution.py:36
  31.7 12.9 %collective-permute-start.17 = (f32[48,128]{1,0:T(8,128)S(1)}, f32[48,128]{1,0:T(8,128)S(1)}, u32[]{:S(2)}, u32[]{:S(2)}) collective-permute-start(f32[48,128]{1,0:T(8,128)S(1)} %get-tuple-element.47), channel_id=1, source_target_pairs={{0,6},{2,0},{4,2},{6,4},{1,7},{3,1},{5,3},{7,5},{8,14},{10,8},{12,... | collective-permute-start | bytes 73736 | tf_op jit(solution)/shard_map/ppermute | solution.py:36
  42.8 21.4 %collective-permute-start.13 = (f32[4,48,128]{2,1,0:T(8,128)S(1)}, f32[4,48,128]{2,1,0:T(8,128)S(1)}, u32[]{:S(2)}, u32[]{:S(2)}) collective-permute-start(f32[4,48,128]{2,1,0:T(8,128)S(1)} %bitcast_dynamic-update-slice_fusion.32), channel_id=1, source_target_pairs={{0,6},{2,0},{4,2},{6,4},{1,7},{3,1},{5,3},{7,5},{8,14},{10,8},{12,... | collective-permute-start | bytes 294920 | tf_op jit(solution)/shard_map/ppermute | solution.py:36
  42.8 21.3 %collective-permute-start.12 = (f32[4,48,128]{2,1,0:T(8,128)S(1)}, f32[4,48,128]{2,1,0:T(8,128)S(1)}, u32[]{:S(2)}, u32[]{:S(2)}) collective-permute-start(f32[4,48,128]{2,1,0:T(8,128)S(1)} %bitcast_dynamic-update-slice_fusion.32), channel_id=1, source_target_pairs={{0,4},{2,6},{4,0},{6,2},{1,5},{3,7},{5,1},{7,3},{8,12},{10,14},{12... | collective-permute-start | bytes 294920 | tf_op jit(solution)/shard_map/ppermute | solution.py:36
  43.1 21.0 %collective-permute-start.11 = (f32[4,48,128]{2,1,0:T(8,128)S(1)}, f32[4,48,128]{2,1,0:T(8,128)S(1)}, u32[]{:S(2)}, u32[]{:S(2)}) collective-permute-start(f32[4,48,128]{2,1,0:T(8,128)S(1)} %bitcast_dynamic-update-slice_fusion.32), channel_id=1, source_target_pairs={{0,2},{2,4},{4,6},{6,0},{1,3},{3,5},{5,7},{7,1},{8,10},{10,12},{12... | collective-permute-start | bytes 294920 | tf_op jit(solution)/shard_map/ppermute | solution.py:36
  44.6 11.7 %collective-permute-start.20 = (f32[4,48,128]{2,1,0:T(8,128)S(1)}, f32[4,48,128]{2,1,0:T(8,128)S(1)}, u32[]{:S(2)}, u32[]{:S(2)}) collective-permute-start(f32[4,48,128]{2,1,0:T(8,128)S(1)} %bitcast_dynamic-update-slice_fusion.28), channel_id=1, source_target_pairs={{0,24},{8,0},{16,8},{24,16},{1,25},{9,1},{17,9},{25,17},{2,26},{10... | collective-permute-start | bytes 294920 | tf_op jit(solution)/shard_map/ppermute | solution.py:36
  92.9 19.7 %all-to-all-start.1 = ((f32[16,16,256]{2,1,0:T(8,128)}), f32[16,16,256]{2,1,0:T(8,128)S(1)}, u32[]{:S(2)}, u32[]{:S(2)}) async-start(f32[16,16,256]{2,1,0:T(8,128)} %broadcast_in_dim.197), calls=%async_computation.1 | async-start | bytes 524288 | tf_op jit(solution)/shard_map/all_to_all | solution.py:51
  119.3 19.5 %all-to-all-start.3 = ((f32[8,48,256]{2,1,0:T(8,128)}), f32[8,48,256]{2,1,0:T(8,128)S(1)}, u32[]{:S(2)}, u32[]{:S(2)}) async-start(f32[8,48,256]{2,1,0:T(8,128)} %bitcast.32), calls=%async_computation.3 | async-start | bytes 786432 | tf_op jit(solution)/shard_map/all_to_all | solution.py:403
  122.8 14.6 %collective-permute-start.22 = (f32[48,256]{1,0:T(8,128)S(1)}, f32[48,256]{1,0:T(8,128)S(1)}, u32[]{:S(2)}, u32[]{:S(2)}) collective-permute-start(f32[48,256]{1,0:T(8,128)S(1)} %add_add_fusion), channel_id=1, source_target_pairs={{0,0},{16,1},{1,2},{17,3},{32,4},{48,5},{33,6},{49,7},{64,8},{80,9... | collective-permute-start | bytes 147464 | tf_op jit(solution)/shard_map/ppermute | solution.py:405
  139.9 28.0 %all-to-all-start.4 = ((f32[8,48,512]{2,1,0:T(8,128)}), f32[8,48,512]{2,1,0:T(8,128)S(1)}, u32[]{:S(2)}, u32[]{:S(2)}) async-start(f32[8,48,512]{2,1,0:T(8,128)} %broadcast_in_dim.199), calls=%async_computation.4 | async-start | bytes 1572864 | tf_op jit(solution)/shard_map/all_to_all | solution.py:51
  170.7 28.4 %collective-permute-start.28 = (f32[48,128]{1,0:T(8,128)S(1)}, f32[48,128]{1,0:T(8,128)S(1)}, u32[]{:S(2)}, u32[]{:S(2)}) collective-permute-start(f32[48,128]{1,0:T(8,128)S(1)} %get-tuple-element.45), channel_id=1, source_target_pairs={{0,4},{2,6},{4,0},{6,2},{1,5},{3,7},{5,1},{7,3},{8,12},{10,14},{12... | collective-permute-start | bytes 73736 | tf_op jit(solution)/shard_map/ppermute | solution.py:36
  177.2 19.2 %collective-permute-start.27 = (f32[48,128]{1,0:T(8,128)S(1)}, f32[48,128]{1,0:T(8,128)S(1)}, u32[]{:S(2)}, u32[]{:S(2)}) collective-permute-start(f32[48,128]{1,0:T(8,128)S(1)} %get-tuple-element.45), channel_id=1, source_target_pairs={{0,2},{2,4},{4,6},{6,0},{1,3},{3,5},{5,7},{7,1},{8,10},{10,12},{12... | collective-permute-start | bytes 73736 | tf_op jit(solution)/shard_map/ppermute | solution.py:36
  177.9 21.1 %collective-permute-start.29 = (f32[48,128]{1,0:T(8,128)S(1)}, f32[48,128]{1,0:T(8,128)S(1)}, u32[]{:S(2)}, u32[]{:S(2)}) collective-permute-start(f32[48,128]{1,0:T(8,128)S(1)} %get-tuple-element.45), channel_id=1, source_target_pairs={{0,6},{2,0},{4,2},{6,4},{1,7},{3,1},{5,3},{7,5},{8,14},{10,8},{12,... | collective-permute-start | bytes 73736 | tf_op jit(solution)/shard_map/ppermute | solution.py:36
  180.5 18.7 %collective-permute-start.25 = (f32[48,128]{1,0:T(8,128)S(1)}, f32[48,128]{1,0:T(8,128)S(1)}, u32[]{:S(2)}, u32[]{:S(2)}) collective-permute-start(f32[48,128]{1,0:T(8,128)S(1)} %get-tuple-element.46), channel_id=1, source_target_pairs={{0,16},{8,24},{16,0},{24,8},{1,17},{9,25},{17,1},{25,9},{2,18},{10... | collective-permute-start | bytes 73736 | tf_op jit(solution)/shard_map/ppermute | solution.py:36
  182.6 16.5 %collective-permute-start.24 = (f32[48,128]{1,0:T(8,128)S(1)}, f32[48,128]{1,0:T(8,128)S(1)}, u32[]{:S(2)}, u32[]{:S(2)}) collective-permute-start(f32[48,128]{1,0:T(8,128)S(1)} %get-tuple-element.46), channel_id=1, source_target_pairs={{0,8},{8,16},{16,24},{24,0},{1,9},{9,17},{17,25},{25,1},{2,10},{10... | collective-permute-start | bytes 73736 | tf_op jit(solution)/shard_map/ppermute | solution.py:36
  189.0 18.6 %all-to-all-start.5 = ((f32[32,8,256]{2,1,0:T(8,128)}), f32[32,8,256]{2,1,0:T(8,128)S(1)}, u32[]{:S(2)}, u32[]{:S(2)}) async-start(f32[32,8,256]{2,1,0:T(8,128)} %convolution_bitcast_fusion), calls=%async_computation.5 | async-start | bytes 524288 | tf_op jit(solution)/shard_map/all_to_all | solution.py:420
  207.7 20.2 %collective-permute-start.32 = (f32[4,48,128]{2,1,0:T(8,128)S(1)}, f32[4,48,128]{2,1,0:T(8,128)S(1)}, u32[]{:S(2)}, u32[]{:S(2)}) collective-permute-start(f32[4,48,128]{2,1,0:T(8,128)S(1)} %bitcast_dynamic-update-slice_fusion.24), channel_id=1, source_target_pairs={{0,6},{2,0},{4,2},{6,4},{1,7},{3,1},{5,3},{7,5},{8,14},{10,8},{12,... | collective-permute-start | bytes 294920 | tf_op jit(solution)/shard_map/ppermute | solution.py:36
  208.9 18.9 %collective-permute-start.31 = (f32[4,48,128]{2,1,0:T(8,128)S(1)}, f32[4,48,128]{2,1,0:T(8,128)S(1)}, u32[]{:S(2)}, u32[]{:S(2)}) collective-permute-start(f32[4,48,128]{2,1,0:T(8,128)S(1)} %bitcast_dynamic-update-slice_fusion.24), channel_id=1, source_target_pairs={{0,4},{2,6},{4,0},{6,2},{1,5},{3,7},{5,1},{7,3},{8,12},{10,14},{12... | collective-permute-start | bytes 294920 | tf_op jit(solution)/shard_map/ppermute | solution.py:36
  208.9 18.9 %collective-permute-start.30 = (f32[4,48,128]{2,1,0:T(8,128)S(1)}, f32[4,48,128]{2,1,0:T(8,128)S(1)}, u32[]{:S(2)}, u32[]{:S(2)}) collective-permute-start(f32[4,48,128]{2,1,0:T(8,128)S(1)} %bitcast_dynamic-update-slice_fusion.24), channel_id=1, source_target_pairs={{0,2},{2,4},{4,6},{6,0},{1,3},{3,5},{5,7},{7,1},{8,10},{10,12},{12... | collective-permute-start | bytes 294920 | tf_op jit(solution)/shard_map/ppermute | solution.py:36
  209.3 17.2 %collective-permute-start.36 = (f32[4,48,128]{2,1,0:T(8,128)S(1)}, f32[4,48,128]{2,1,0:T(8,128)S(1)}, u32[]{:S(2)}, u32[]{:S(2)}) collective-permute-start(f32[4,48,128]{2,1,0:T(8,128)S(1)} %bitcast_dynamic-update-slice_fusion.20), channel_id=1, source_target_pairs={{0,24},{8,0},{16,8},{24,16},{1,25},{9,1},{17,9},{25,17},{2,26},{10... | collective-permute-start | bytes 294920 | tf_op jit(solution)/shard_map/ppermute | solution.py:36
  211.6 20.3 %all-to-all-start.6 = ((f32[32,8,256]{2,1,0:T(8,128)}), f32[32,8,256]{2,1,0:T(8,128)S(1)}, u32[]{:S(2)}, u32[]{:S(2)}) async-start(f32[32,8,256]{2,1,0:T(8,128)} %broadcast_in_dim.220), calls=%async_computation.6 | async-start | bytes 524288 | tf_op jit(solution)/shard_map/all_to_all | solution.py:51
  (28 other events, 188.5 us)
